TPU v7x, 32 devices: a whole 2x2x4 slice. The times are simulated.
32 devices in a mesh: img: 4 (over y, x), seq: 8 (over z, core).
Axes of the slice: x: 2, y: 2, z: 4, core: 2. Of those that a mesh axis runs over, the one named last changes fastest.
Arguments:
- image_query: bfloat16 [4, 1024, 1280], P('img', 'seq'), may hold values from -7 to 7
- image_key: bfloat16 [4, 1024, 1280], P('img', 'seq'), may hold values from -7 to 7
- image_value: bfloat16 [4, 1024, 1280], P('img', 'seq'), may hold values from -3 to 3
- image_output: bfloat16 [4, 1024, 1280], P('img', 'seq'), may hold values from -0.875 to 0.875
- output_grad: bfloat16 [4, 1024, 2432], P('img', 'seq'), may hold values from -48 to 48
- image_logsum: float32 [4, 1024, 20], P('img', 'seq'), may hold values from 8 to 9
- text_query: bfloat16 [4, 333, 1280], P('img'), may hold values from -7 to 7
- text_key: bfloat16 [4, 333, 1280], P('img'), may hold values from -7 to 7
- text_value: bfloat16 [4, 333, 1280], P('img'), may hold values from -3 to 3
- text_output: bfloat16 [4, 333, 1280], P('img'), may hold values from -0.875 to 0.875
- text_grad: bfloat16 [4, 333, 1280], P('img'), may hold values from -48 to 48
- text_logsum: float32 [4, 333, 20], P('img'), may hold values from 8 to 9
- out_weight: bfloat16 [2432, 1280], replicated, may hold values from -0.125 to 0.125
Outputs:
- query_grad: bfloat16 [4, 1024, 1280], P('img', 'seq')
- key_grad: bfloat16 [4, 1024, 1280], P('img', 'seq')
- value_grad: bfloat16 [4, 1024, 1280], P('img', 'seq')
- text_query_grad: bfloat16 [4, 333, 1280], P('img')
- text_key_grad: bfloat16 [4, 333, 1280], P('img')
- text_value_grad: bfloat16 [4, 333, 1280], P('img')
- weight_grad: float32 [2432, 1280], P('seq')
All inputs are finite; a program needn't handle non-finite values.
Results may differ from a plain program's by a relative error of at most 0.017.
Values may be sent and summed in bfloat16 or wider, within the bound.
A program may use at most 192 MiB of HBM per device.

v0:
```python
import functools

import jax
import jax.numpy as jnp
from jax import lax
from jax.experimental import pallas as pl
from jax.experimental.pallas import tpu as pltpu
from jax.sharding import PartitionSpec as P

LANES = 128
SUB = 16
MESH = pl.DeviceIdType.MESH
NN = (((1,), (0,)), ((), ()))
NT = (((1,), (1,)), ((), ()))
TN = (((0,), (0,)), ((), ()))
BF = jnp.bfloat16
F32 = jnp.float32


def up(value, step):
    return -(-value // step) * step


class Plan:
    def __init__(self, peers, images, rows, text_rows, model, feature, heads):
        self.peers, self.images, self.rows = peers, images, rows
        self.text_rows, self.model, self.feature, self.heads = text_rows, model, feature, heads
        self.chips = peers // 2
        self.width = feature // heads
        self.depth = 2 * self.width
        self.most = -(-heads // peers)
        self.stat_rows = up(2 * self.most, 8)
        self.tokens = peers * rows
        self.total = self.tokens + up(text_rows, LANES)
        self.key_block = self.total // 8
        self.text_even = up(text_rows, SUB)
        self.text_half = up(self.text_even // 2, SUB)
        self.out_rows = rows + rows // 2
        self.out_text = self.text_even + self.text_half
        self.share = model // peers
        self.share_pad = up(self.share, SUB)
        self.part = up(-(-self.share_pad // images), SUB)

    def first(self, device):
        return device * self.heads // self.peers

    def part_start(self, image):
        if isinstance(image, int):
            return min(image * self.part, self.share_pad - self.part)
        return pl.multiple_of(jnp.minimum(image * self.part, self.share_pad - self.part), SUB)


def exchange_kernel(
    plan,
    q_ref, k_ref, v_ref, o_ref, og_ref, ls_ref,
    tq_ref, tk_ref, tv_ref, to_ref, tg_ref, tls_ref, w_ref,
    back_ref, tback_ref, parts_ref,
    w_s, txt_s, qk_out, gv_out, st_out, x_qk, x_gv, st_in, st_text, dots_s, tdots_s, stat_s,
    q_s, k_s, v_s, g_s, dk_s, dv_s, dq_s, result_s, ogt_s, og_in, io_in, sums_out, sums_in,
    local_sem, qk_send, qk_recv, gv_send, gv_recv, st_send, st_recv, back_send, back_recv,
    text_send, text_recv, io_send, io_recv, og_send, og_recv, sums_send, sums_recv,
    parts_send, parts_recv,
):
    p = plan
    peers, images, rows, width, depth, chips = p.peers, p.images, p.rows, p.width, p.depth, p.chips
    scaling = width ** (-0.5)
    me = lax.axis_index("seq")
    image = lax.axis_index("img")
    chip, core = me // 2, me % 2
    first = p.first(me)
    count = p.first(me + 1) - first
    slot = image * 2 + core
    my_rows = pl.ds(pl.multiple_of(me * rows, rows), rows)

    def remote(source, target, send, recv, device):
        return pltpu.make_async_remote_copy(
            src_ref=source, dst_ref=target, send_sem=send, recv_sem=recv,
            device_id=device, device_id_type=MESH,
        )

    loads = [
        pltpu.make_async_copy(ref, txt_s.at[number], local_sem.at[number])
        for number, ref in enumerate((tq_ref, tk_ref, tv_ref, tg_ref, to_ref))
    ]
    load_w = pltpu.make_async_copy(w_ref, w_s, local_sem.at[5])
    load_w.start()
    for load in loads:
        load.start()

    barrier = pltpu.get_barrier_semaphore()

    @pl.loop(1, peers)
    def _(step):
        pl.semaphore_signal(barrier, inc=1, device_id=(image, (me + step) % peers), device_id_type=MESH)

    @pl.loop(1, images)
    def _(step):
        for side in range(2):
            pl.semaphore_signal(
                barrier, inc=1, device_id=((image + step) % images, chip * 2 + side), device_id_type=MESH
            )

    for head in range(p.heads):
        cols = slice(head * width, (head + 1) * width)
        qk_out[head] = jnp.concatenate([q_ref[:, cols] * jnp.asarray(scaling, BF), k_ref[:, cols]], axis=1)

    pl.semaphore_wait(barrier, peers - 1 + 2 * (images - 1))

    def targets(j, action):
        @pl.loop(0, peers)
        def _(step):
            device = (me + peers // 2 + step) % peers
            head = p.first(device) + j

            @pl.when((device != me) & (head < p.first(device + 1)))
            def _():
                action(device, head)

    def copy_qk(j):
        return lambda device, head: remote(
            qk_out.at[head], x_qk.at[j, my_rows], qk_send.at[head], qk_recv.at[j], (image, device)
        )

    def copy_gv(j):
        return lambda device, head: remote(
            gv_out.at[head], x_gv.at[j, my_rows], gv_send.at[head], gv_recv.at[j], (image, device)
        )

    def copy_st(device):
        return remote(st_out.at[device], st_in.at[me], st_send.at[device], st_recv.at[me], (image, device))

    targets(0, lambda device, head: copy_qk(0)(device, head).start())

    def copy_io(step):
        return remote(
            o_ref, io_in.at[slot], io_send.at[step], io_recv.at[slot], ((image + step) % images, me)
        )

    def share_io(step):
        source = ((image + step) % images) * 2 + core
        return remote(
            io_in.at[source], io_in.at[source], io_send.at[images + step], io_recv.at[source],
            (image, chip * 2 + 1 - core),
        )

    copy_own = remote(
        o_ref, io_in.at[slot], io_send.at[0], io_recv.at[slot], (image, chip * 2 + 1 - core)
    )

    @pl.loop(1, images)
    def _(step):
        copy_io(step).start()

    copy_own.start()

    for number in range(-(-p.model // LANES)):
        lanes = slice(number * LANES, (number + 1) * LANES)
        dq_s[:, 0:rows] = jnp.zeros((LANES, rows), F32) + og_ref[:, lanes].astype(F32).T
        turned = dq_s[:, 0:rows]
        for device in range(peers):
            low = max(number * LANES, device * p.share)
            high = min((number + 1) * LANES, (device + 1) * p.share)
            if low < high:
                ogt_s[device % 2, device // 2, low - device * p.share : high - device * p.share, :] = turned[
                    low - number * LANES : high - number * LANES
                ].astype(BF)

    def copy_og(step, side):
        other = (image + step) % images
        return remote(
            ogt_s.at[side, :, pl.ds(p.part_start(other), p.part)],
            og_in.at[:, :, pl.ds(pl.multiple_of(slot * rows, rows), rows)],
            og_send.at[step, side],
            og_recv.at[slot],
            (other, chip * 2 + side),
        )

    @pl.loop(1, images)
    def _(step):
        for side in range(2):
            copy_og(step, side).start()

    for side in range(2):
        @pl.when(core != side)
        def _():
            copy_og(0, side).start()

    og_in[:, :, pl.ds(pl.multiple_of(slot * rows, rows), rows)] = ogt_s[
        core, :, pl.ds(p.part_start(image), p.part)
    ]
    io_in[slot] = o_ref[...]

    load_w.wait()

    @pl.loop(0, p.feature // 256)
    def _(step):
        lanes = pl.ds(pl.multiple_of(step * 256, 256), 256)
        g_cols = jnp.dot(og_ref[...], w_s[:, lanes], preferred_element_type=F32).astype(BF)
        per = 256 // width
        for number in range(per):
            head = step * per + number
            gv_out[head, :, 0:width] = g_cols[:, number * width : (number + 1) * width]

    pick_rows = up(p.heads, 8)
    tag = lax.broadcasted_iota(jnp.int32, (pick_rows, p.feature), 0)
    lane_at = lax.broadcasted_iota(jnp.int32, (pick_rows, p.feature), 1)
    picker = jnp.where((lane_at >= tag * width) & (lane_at < (tag + 1) * width), 1.0, 0.0).astype(F32)

    def row_dots(grads, outputs):
        product = grads.astype(F32) * outputs.astype(F32)
        return lax.dot_general(
            picker, product, NT, precision=lax.Precision.HIGHEST, preferred_element_type=F32
        )

    gathered = jnp.concatenate([gv_out[head, :, 0:width] for head in range(p.heads)], axis=1)
    dots_s[...] = row_dots(gathered, o_ref[...])
    for head in range(p.heads):
        gv_out[head, :, width:depth] = v_ref[:, head * width : (head + 1) * width]
    st_out[...] = jnp.zeros_like(st_out)
    for device in range(peers):
        for j in range(p.first(device + 1) - p.first(device)):
            head = p.first(device) + j
            st_out[device, 2 * j : 2 * j + 1, :] = -ls_ref[head : head + 1, :]
            st_out[device, 2 * j + 1 : 2 * j + 2, :] = -dots_s[head : head + 1, :]

    @pl.loop(0, peers)
    def _(step):
        device = (me + peers // 2 + step) % peers

        @pl.when(device != me)
        def _():
            copy_st(device).start()

    targets(0, lambda device, head: copy_gv(0)(device, head).start())
    for j in range(1, p.most):
        targets(j, lambda device, head: copy_qk(j)(device, head).start())
        targets(j, lambda device, head: copy_gv(j)(device, head).start())

    for load in loads:
        load.wait()
    tdots_s[...] = row_dots(txt_s[3], txt_s[4])
    st_text[...] = jnp.zeros_like(st_text)
    text_at = slice(p.tokens, p.tokens + p.text_rows)
    pad_at = slice(p.tokens + p.text_rows // SUB * SUB, p.total)

    @pl.loop(0, count)
    def _(j):
        head = first + j
        tile = pl.ds(pl.multiple_of(head // 2 * depth, depth), depth)
        odd = head % 2 == 1

        def text_cols(number):
            value = txt_s[number, :, tile]
            return jnp.where(odd, value[:, width:], value[:, :width])

        x_qk[j, my_rows] = qk_out[head]
        x_gv[j, my_rows] = gv_out[head]
        x_qk[j, pad_at] = jnp.zeros((p.total - pad_at.start, depth), BF)
        x_gv[j, pad_at] = jnp.zeros((p.total - pad_at.start, depth), BF)
        x_qk[j, text_at] = jnp.concatenate([text_cols(0) * jnp.asarray(scaling, BF), text_cols(1)], axis=1)
        x_gv[j, text_at] = jnp.concatenate([text_cols(3), text_cols(2)], axis=1)
        st_text[pl.ds(2 * j, 1), 0 : p.text_rows] = -tls_ref[pl.ds(head, 1), :]
        st_text[pl.ds(2 * j + 1, 1), 0 : p.text_rows] = -tdots_s[pl.ds(head, 1), :]

    def stats_tile(value):
        terms = []
        for _ in range(3):
            term = value.astype(BF).astype(F32)
            terms.append(term)
            value = value - term
        used = width + 3 * p.stat_rows
        return jnp.concatenate(
            [jnp.zeros((width, LANES), F32), *terms, jnp.zeros((depth - used, LANES), F32)], axis=0
        ).T.astype(BF)

    for number in range((p.total - p.tokens) // LANES):
        stat_s[p.tokens + number * LANES : p.tokens + (number + 1) * LANES, :] = stats_tile(
            st_text[:, number * LANES : (number + 1) * LANES]
        )

    st_in[me] = st_out[me]

    @pl.loop(1, peers)
    def _(step):
        source = (me + step) % peers
        remote(st_out.at[0], st_in.at[source], st_send.at[0], st_recv.at[source], (image, source)).wait_recv()

    @pl.loop(0, peers)
    def _(source):
        stat_s[pl.ds(pl.multiple_of(source * rows, rows), rows), :] = stats_tile(st_in[source])

    lane = lax.broadcasted_iota(jnp.int32, (p.total, depth), 1)

    def ones(start):
        inside = (lane == width + start)
        for number in range(1, 3):
            inside = inside | (lane == width + start + number * p.stat_rows)
        return jnp.where(inside, 1.0, 0.0).astype(BF)[:, width:]

    far = pl.ds(0, (peers - 1) * rows)

    def text_copy(head, way, device):
        return remote(
            tback_ref.at[head], tback_ref.at[head], text_send.at[head, way], text_recv.at[head], (image, device)
        )

    def send_text(head, upward, downward):
        @pl.when(upward & (chip + 1 < chips))
        def _():
            text_copy(head, 0, me + 2).start()

        @pl.when(downward & (chip > 0))
        def _():
            text_copy(head, 1, me - 2).start()

        text_copy(head, 2, chip * 2 + 1 - core).start()

    @pl.loop(0, count)
    def _(j):
        head = first + j
        pltpu.make_async_copy(x_qk.at[j, far], x_qk.at[j, far], qk_recv.at[j]).wait()
        pltpu.make_async_copy(x_gv.at[j, far], x_gv.at[j, far], gv_recv.at[j]).wait()
        both = x_qk[j]
        q_s[...] = jnp.where(lane < width, both, stat_s[...])
        k_s[...] = jnp.concatenate([both[:, width:], ones(2 * j)], axis=1)
        both = x_gv[j]
        g_s[...] = jnp.where(lane < width, both, stat_s[...])
        v_s[...] = jnp.concatenate([both[:, width:], ones(2 * j + 1)], axis=1)
        dq_s[...] = jnp.zeros_like(dq_s)

        @pl.loop(0, p.total // p.key_block)
        def _(step):
            at = pl.ds(pl.multiple_of(step * p.key_block, p.key_block), p.key_block)
            keys = k_s[at, :]
            scores = lax.dot_general(keys, q_s[...], NT, preferred_element_type=F32)
            weights = jnp.exp(scores)
            grads = lax.dot_general(v_s[at, :], g_s[...], NT, preferred_element_type=F32)
            low = (weights * grads).astype(BF)
            dv_s[at, :] = jnp.dot(weights.astype(BF), g_s[...], preferred_element_type=F32).astype(BF)
            dk_s[at, :] = jnp.dot(low, q_s[...], preferred_element_type=F32).astype(BF)
            dq_s[...] += lax.dot_general(keys, low, TN, preferred_element_type=F32)

        @pl.loop(0, peers)
        def _(block):
            base = pl.multiple_of(block * rows, rows)
            dq = (dq_s[:, pl.ds(base, rows)].T * scaling).astype(BF)
            top = jnp.concatenate([dq[:, :width], dk_s[pl.ds(base, rows), :width]], axis=1)
            dv = dv_s[pl.ds(base, rows), :width]
            bottom = jnp.concatenate([dv[: rows // 2], dv[rows // 2 :]], axis=1)
            result_s[j, block, 0:rows] = top
            result_s[j, block, rows : p.out_rows] = bottom

            @pl.when(block == me)
            def _():
                back_ref[head, 0:rows] = top
                back_ref[head, rows : p.out_rows] = bottom

            @pl.when(block != me)
            def _():
                remote(
                    result_s.at[j, block], back_ref.at[head], back_send.at[j, block], back_recv.at[head],
                    (image, block),
                ).start()

        dq = (dq_s[:, p.tokens : p.total].T * scaling).astype(BF)
        even, half = p.text_even, p.text_half
        tback_ref[head, 0:even] = jnp.concatenate(
            [dq[:even, :width], dk_s[p.tokens : p.tokens + even, :width]], axis=1
        )
        tback_ref[head, even : even + half] = jnp.concatenate(
            [dv_s[p.tokens : p.tokens + half, :width], dv_s[p.tokens + half : p.tokens + 2 * half, :width]],
            axis=1,
        )
        send_text(head, True, True)

        @pl.when(j == 0)
        def _():
            @pl.loop(1, images)
            def _(step):
                source = ((image + step) % images) * 2 + core
                pltpu.make_async_copy(io_in.at[source], io_in.at[source], io_recv.at[source]).wait()
                share_io(step).start()

        @pl.when(j == jnp.minimum(1, count - 1))
        def _():
            @pl.loop(0, images)
            def _(index):
                source = index * 2 + 1 - core
                pltpu.make_async_copy(io_in.at[source], io_in.at[source], io_recv.at[source]).wait()

            @pl.loop(1, 2 * images)
            def _(step):
                source = (slot + step) % (2 * images)
                piece = og_in.at[:, :, pl.ds(pl.multiple_of(source * rows, rows), rows)]
                pltpu.make_async_copy(piece, piece, og_recv.at[source]).wait()

            @pl.loop(0, p.feature // 256)
            def _(step):
                lanes = pl.ds(pl.multiple_of(step * 256, 256), 256)
                for number in range(chips):
                    total = jnp.zeros((p.part, 256), F32)
                    for source in range(2 * images):
                        total += jnp.dot(
                            og_in[number, :, source * rows : (source + 1) * rows],
                            io_in[source, :, lanes],
                            preferred_element_type=F32,
                        )
                    sums_out[number, :, lanes] = total.astype(BF)

            @pl.loop(0, chips)
            def _(number):
                @pl.when(number != chip)
                def _():
                    remote(
                        sums_out.at[number], sums_in.at[chip], sums_send.at[number], sums_recv.at[chip],
                        (image, number * 2 + core),
                    ).start()

            sums_in[chip] = sums_out[chip]

    @pl.loop(1, chips)
    def _(hop):
        for upward in (True, False):
            source = chip - hop if upward else chip + hop

            @pl.when((source >= 0) & (source < chips))
            def _():
                owner = source * 2 + core
                start = p.first(owner)

                @pl.loop(start, p.first(owner + 1))
                def _(head):
                    pltpu.make_async_copy(tback_ref.at[head], tback_ref.at[head], text_recv.at[head]).wait()
                    send_text(head, upward, not upward)

    @pl.loop(1, chips)
    def _(step):
        source = (chip + step) % chips
        pltpu.make_async_copy(sums_in.at[source], sums_in.at[source], sums_recv.at[source]).wait()

    @pl.loop(0, p.feature // 256)
    def _(step):
        lanes = pl.ds(pl.multiple_of(step * 256, 256), 256)
        total = sums_in[0, :, lanes].astype(F32)
        for source in range(1, chips):
            total += sums_in[source, :, lanes].astype(F32)
        parts_ref[image, :, lanes] = total.astype(BF)

    def copy_parts(step):
        return remote(
            parts_ref.at[image], parts_ref.at[image], parts_send.at[step], parts_recv.at[image],
            ((image + step) % images, me),
        )

    @pl.loop(1, images)
    def _(step):
        copy_parts(step).start()

    @pl.loop(0, p.heads)
    def _(head):
        @pl.when((head < first) | (head >= first + count))
        def _():
            pltpu.make_async_copy(back_ref.at[head], back_ref.at[head], back_recv.at[head]).wait()
            pltpu.make_async_copy(qk_out.at[head], qk_out.at[head], qk_send.at[head]).wait()
            pltpu.make_async_copy(gv_out.at[head], gv_out.at[head], gv_send.at[head]).wait()

    @pl.loop(0, chips)
    def _(number):
        owner = number * 2 + 1 - core

        @pl.loop(p.first(owner), p.first(owner + 1))
        def _(head):
            pltpu.make_async_copy(tback_ref.at[head], tback_ref.at[head], text_recv.at[head]).wait()

        owner = number * 2 + core

        @pl.loop(p.first(owner), p.first(owner + 1))
        def _(head):
            @pl.when((number <= chip) & (chip + 1 < chips))
            def _():
                text_copy(head, 0, me).wait_send()

            @pl.when((number >= chip) & (chip > 0))
            def _():
                text_copy(head, 1, me).wait_send()

            text_copy(head, 2, me).wait_send()

        @pl.when(number != chip)
        def _():
            pltpu.make_async_copy(sums_out.at[number], sums_out.at[number], sums_send.at[number]).wait()

    @pl.loop(0, peers)
    def _(device):
        @pl.when(device != me)
        def _():
            pltpu.make_async_copy(st_out.at[device], st_out.at[device], st_send.at[device]).wait()

            @pl.loop(0, count)
            def _(j):
                piece = result_s.at[j, device]
                pltpu.make_async_copy(piece, piece, back_send.at[j, device]).wait()

    copy_own.wait_send()
    for side in range(2):
        @pl.when(core != side)
        def _():
            copy_og(0, side).wait_send()

    @pl.loop(1, images)
    def _(step):
        copy_io(step).wait_send()
        share_io(step).wait_send()
        copy_parts(step).wait_send()
        for side in range(2):
            copy_og(step, side).wait_send()
        source = (image + step) % images
        pltpu.make_async_copy(parts_ref.at[source], parts_ref.at[source], parts_recv.at[source]).wait()


def exchange(plan, *arrays):
    p = plan
    dma = pltpu.SemaphoreType.DMA
    vmem = pl.BlockSpec(memory_space=pltpu.VMEM)
    anywhere = pl.BlockSpec(memory_space=pl.ANY)
    pick = up(p.heads, 8)
    wide = (p.total, p.depth)
    return pl.pallas_call(
        functools.partial(exchange_kernel, p),
        out_shape=(
            jax.ShapeDtypeStruct((p.heads, p.out_rows, p.depth), BF),
            jax.ShapeDtypeStruct((p.heads, p.out_text, p.depth), BF),
            jax.ShapeDtypeStruct((p.images, p.part, p.feature), BF),
        ),
        in_specs=[vmem] * 6 + [anywhere] * 5 + [vmem, anywhere],
        out_specs=(vmem,) * 3,
        scratch_shapes=[
            pltpu.VMEM((p.model, p.feature), BF),
            pltpu.VMEM((5, p.text_rows, p.feature), BF),
            pltpu.VMEM((p.heads, p.rows, p.depth), BF),
            pltpu.VMEM((p.heads, p.rows, p.depth), BF),
            pltpu.VMEM((p.peers, p.stat_rows, p.rows), F32),
            pltpu.VMEM((p.most, *wide), BF),
            pltpu.VMEM((p.most, *wide), BF),
            pltpu.VMEM((p.peers, p.stat_rows, p.rows), F32),
            pltpu.VMEM((p.stat_rows, p.total - p.tokens), F32),
            pltpu.VMEM((pick, p.rows), F32),
            pltpu.VMEM((pick, p.text_rows), F32),
            pltpu.VMEM(wide, BF),
        ]
        + [pltpu.VMEM(wide, BF)] * 6
        + [
            pltpu.VMEM((p.depth, p.total), F32),
            pltpu.VMEM((p.most, p.peers, p.out_rows, p.depth), BF),
            pltpu.VMEM((2, p.chips, p.share_pad, p.rows), BF),
            pltpu.VMEM((p.chips, p.part, 2 * p.images * p.rows), BF),
            pltpu.VMEM((2 * p.images, p.rows, p.feature), BF),
            pltpu.VMEM((p.chips, p.part, p.feature), BF),
            pltpu.VMEM((p.chips, p.part, p.feature), BF),
            dma((6,)),
            dma((p.heads,)), dma((p.most,)),
            dma((p.heads,)), dma((p.most,)),
            dma((p.peers,)), dma((p.peers,)),
            dma((p.most, p.peers)), dma((p.heads,)),
            dma((p.heads, 3)), dma((p.heads,)),
            dma((2 * p.images,)), dma((2 * p.images,)),
            dma((p.images, 2)), dma((2 * p.images,)),
            dma((p.chips,)), dma((p.chips,)),
            dma((p.images,)), dma((p.images,)),
        ],
        compiler_params=pltpu.CompilerParams(
            collective_id=0, has_side_effects=True, vmem_limit_bytes=60 << 20
        ),
    )(*arrays)


def finish_kernel(plan, back_ref, tback_ref, parts_ref, dq_ref, dk_ref, dv_ref, tdq_ref, tdk_ref, tdv_ref, wg_ref):
    p = plan
    width, rows, half, even = p.width, p.rows, p.text_half, p.text_even
    for pair in range(p.heads // 2):
        lanes = slice(pair * p.depth, (pair + 1) * p.depth)

        def join(ref, at, cols):
            return jnp.concatenate([ref[2 * pair, at, cols], ref[2 * pair + 1, at, cols]], axis=1)

        left, right = slice(0, width), slice(width, p.depth)
        dq_ref[:, lanes] = join(back_ref, slice(0, rows), left)
        dk_ref[:, lanes] = join(back_ref, slice(0, rows), right)
        dv_ref[0 : rows // 2, lanes] = join(back_ref, slice(rows, p.out_rows), left)
        dv_ref[rows // 2 : rows, lanes] = join(back_ref, slice(rows, p.out_rows), right)
        tdq_ref[:, lanes] = join(tback_ref, slice(0, p.text_rows), left)
        tdk_ref[:, lanes] = join(tback_ref, slice(0, p.text_rows), right)
        tdv_ref[0:half, lanes] = join(tback_ref, slice(even, even + half), left)
        tdv_ref[half : p.text_rows, lanes] = join(tback_ref, slice(even, even + p.text_rows - half), right)
    for number in range(p.images):
        start = p.part_start(number)
        stop = min(start + p.part, p.share)
        wg_ref[start:stop, :] = parts_ref[number, 0 : stop - start, :].astype(F32)


def finish(plan, back, tback, parts):
    p = plan
    vmem = pl.BlockSpec(memory_space=pltpu.VMEM)
    token = jax.ShapeDtypeStruct((p.rows, p.feature), BF)
    text = jax.ShapeDtypeStruct((p.text_rows, p.feature), BF)
    return pl.pallas_call(
        functools.partial(finish_kernel, p),
        out_shape=(token,) * 3 + (text,) * 3 + (jax.ShapeDtypeStruct((p.share, p.feature), F32),),
        in_specs=[vmem] * 3,
        out_specs=(vmem,) * 7,
        compiler_params=pltpu.CompilerParams(vmem_limit_bytes=40 << 20),
    )(back, tback, parts)


def shards(
    image_query,
    image_key,
    image_value,
    image_output,
    output_grad,
    image_logsum,
    text_query,
    text_key,
    text_value,
    text_output,
    text_grad,
    text_logsum,
    out_weight,
):
    plan = Plan(
        lax.axis_size("seq"),
        lax.axis_size("img"),
        image_query.shape[1],
        text_query.shape[1],
        output_grad.shape[2],
        image_query.shape[2],
        image_logsum.shape[2],
    )
    results = exchange(
        plan,
        image_query[0], image_key[0], image_value[0], image_output[0], output_grad[0], image_logsum[0].T,
        text_query[0], text_key[0], text_value[0], text_output[0], text_grad[0], text_logsum[0].T,
        out_weight,
    )
    *grads, weight_grad = finish(plan, *results)
    return (*(grad[None] for grad in grads), weight_grad)


def solution(mesh):
    token = P("img", "seq", None)
    text = P("img", None, None)
    return jax.shard_map(
        shards,
        mesh=mesh,
        in_specs=(token,) * 6 + (text,) * 6 + (P(),),
        out_specs=(token,) * 3 + (text,) * 3 + (P("seq", None),),
        check_vma=False,
    )
```

profile of v0, /device:TPU:1, one launch (start us, length us, event | category | flops | bytes accessed | tf_op | source)
XLA Modules:
  0.0 116.0 jit_solution(16537438037229478113)
XLA Ops:
  0.6 1.3 %copy.25 = f32[1,128,20]{1,2,0:T(8,128)} copy(f32[1,128,20]{1,0,2:T(1,128)} %param.18) | data formatting | bytes 20480
  1.9 1.4 %copy.24 = f32[1,333,20]{1,2,0:T(8,128)} copy(f32[1,333,20]{1,0,2:T(1,128)} %param.24) | data formatting | bytes 53280
  3.3 105.4 %shard_map.180 = (bf16[20,192,128]{2,1,0:T(8,128)(2,1)}, bf16[20,512,128]{2,1,0:T(8,128)(2,1)}, bf16[4,80,1280]{2,1,0:T(8,128)(2,1)}) custom-call(bf16[128,1280]{1,0:T(8,128)(2,1)} %bitcast.32, bf16[128,1280]{1,0:T(8,128)(2,1)} %bitcast.33, bf16[128,1280]{1,0:T(8,128)(2,1)} %bitcast.34, bf16[128,1280]{1,0:T(8,128)(2,1)} %bitcast.35, ...), custom_call_target="tpu_custom_call" | custom-call | tf_op jit(solution)/shard_map/pallas_call | solution.py:528
  108.7 0.0 copy-start
  108.7 1.7 %copy-done = bf16[20,512,128]{2,1,0:T(8,128)(2,1)S(1)} copy-done((bf16[20,512,128]{2,1,0:T(8,128)(2,1)S(1)}, bf16[20,512,128]{2,1,0:T(8,128)(2,1)}, u32[]{:S(2)}) %copy-start) | copy-done | bytes 2621464
  110.4 0.0 copy-start.1
  110.4 1.2 %copy-done.1 = bf16[20,192,128]{2,1,0:T(8,128)(2,1)S(1)} copy-done((bf16[20,192,128]{2,1,0:T(8,128)(2,1)S(1)}, bf16[20,192,128]{2,1,0:T(8,128)(2,1)}, u32[]{:S(2)}) %copy-start.1) | copy-done | bytes 983064
  111.6 0.0 copy-start.2
  111.6 1.1 copy-done.2
  112.8 3.2 %shard_map.181 = (bf16[128,1280]{1,0:T(8,128)(2,1)}, bf16[128,1280]{1,0:T(8,128)(2,1)}, bf16[128,1280]{1,0:T(8,128)(2,1)}, bf16[333,1280]{1,0:T(8,128)(2,1)}, bf...) custom-call(bf16[20,192,128]{2,1,0:T(8,128)(2,1)S(1)} %copy-done.1, ...), custom_call_target="tpu_custom_call" | custom-call | tf_op jit(solution)/shard_map/pallas_call | solution.py:606
Async XLA Ops:
  108.7 1.7 %copy-start = (bf16[20,512,128]{2,1,0:T(8,128)(2,1)S(1)}, bf16[20,512,128]{2,1,0:T(8,128)(2,1)}, u32[]{:S(2)}) copy-start(bf16[20,512,128]{2,1,0:T(8,128)(2,1)} %get-tuple-element.18.tback_ref) | copy-start | bytes 7864324
  110.4 1.2 %copy-start.1 = (bf16[20,192,128]{2,1,0:T(8,128)(2,1)S(1)}, bf16[20,192,128]{2,1,0:T(8,128)(2,1)}, u32[]{:S(2)}) copy-start(bf16[20,192,128]{2,1,0:T(8,128)(2,1)} %get-tuple-element.17.back_ref) | copy-start | bytes 2949124
  111.6 1.1 copy-start.2
where the time goes:
time: 116 us
  Pallas kernels  109 us (94%)
  local copies, waits for them, and re-layouts  6.75 us (6%)
    pallas_call x1, Pallas kernels, exchange(): pl.pallas_call(functools.partial(exchange_kernel, p), out_shape=(jax.Shap...  105 us
    unnamed x8, local copies, waits for them, and re-layouts  6.75 us
    pallas_call x1, Pallas kernels, finish(): pl.pallas_call(functools.partial(finish_kernel, p), out_shape=(token,) *...  3.22 us

commit v1 on v0

--- a/solution.py
+++ b/solution.py
@@ -38,6 +38,7 @@
         self.out_rows = rows + rows // 2
         self.out_text = self.text_even + self.text_half
         self.share = model // peers
+        self.finish_steps = next(n for n in (5, 4, 3, 2, 1) if heads % (2 * n) == 0)
         self.share_pad = up(self.share, SUB)
         self.part = up(-(-self.share_pad // images), SUB)
 
@@ -52,13 +53,13 @@
 
 def exchange_kernel(
     plan,
-    q_ref, k_ref, v_ref, o_ref, og_ref, ls_ref,
-    tq_ref, tk_ref, tv_ref, to_ref, tg_ref, tls_ref, w_ref,
+    q_in, k_in, v_in, o_in, og_in_ref, ls_in,
+    tq_ref, tk_ref, tv_ref, to_ref, tg_ref, tls_in, w_ref,
     back_ref, tback_ref, parts_ref,
-    w_s, txt_s, qk_out, gv_out, st_out, x_qk, x_gv, st_in, st_text, dots_s, tdots_s, stat_s,
-    q_s, k_s, v_s, g_s, dk_s, dv_s, dq_s, result_s, ogt_s, og_in, io_in, sums_out, sums_in,
-    local_sem, qk_send, qk_recv, gv_send, gv_recv, st_send, st_recv, back_send, back_recv,
-    text_send, text_recv, io_send, io_recv, og_send, og_recv, sums_send, sums_recv,
+    q_ref, k_ref, v_ref, o_ref, og_ref, ls_ref, tls_ref, text_s, w_s, txt_s, qk_out, gv_out, st_out, x_qk, x_gv, st_in, st_text, dots_s, tdots_s, stat_s,
+    q_s, k_s, v_s, g_s, dk_s, dv_s, dq_s, result_s, ogt_s, og_in, io_in, sums_out, sums_in, gate_in,
+    local_sem, own_sem, qk_send, qk_recv, gv_send, gv_recv, st_send, st_recv, back_send, back_recv,
+    text_send, text_recv, io_send, io_recv, og_send, og_recv, sums_send, sums_recv, gate_recv,
     parts_send, parts_recv,
 ):
     p = plan
@@ -78,15 +79,6 @@
             device_id=device, device_id_type=MESH,
         )
 
-    loads = [
-        pltpu.make_async_copy(ref, txt_s.at[number], local_sem.at[number])
-        for number, ref in enumerate((tq_ref, tk_ref, tv_ref, tg_ref, to_ref))
-    ]
-    load_w = pltpu.make_async_copy(w_ref, w_s, local_sem.at[5])
-    load_w.start()
-    for load in loads:
-        load.start()
-
     barrier = pltpu.get_barrier_semaphore()
 
     @pl.loop(1, peers)
@@ -99,6 +91,20 @@
             pl.semaphore_signal(
                 barrier, inc=1, device_id=((image + step) % images, chip * 2 + side), device_id_type=MESH
             )
+
+    names = ("q", "k", "o", "og", "w", "v", "ls", "tq", "tk", "tv", "tg", "to", "tls")
+    pairs = (
+        (q_in, q_ref), (k_in, k_ref), (o_in, o_ref), (og_in_ref, og_ref), (w_ref, w_s), (v_in, v_ref), (ls_in, ls_ref),
+        (tq_ref, txt_s.at[0]), (tk_ref, txt_s.at[1]), (tv_ref, txt_s.at[2]), (tg_ref, txt_s.at[3]),
+        (to_ref, txt_s.at[4]), (tls_in, tls_ref),
+    )
+    loads = {}
+    for number, (name, (source, target)) in enumerate(zip(names, pairs)):
+        loads[name] = pltpu.make_async_copy(source, target, local_sem.at[number])
+        loads[name].start()
+
+    loads["q"].wait()
+    loads["k"].wait()
 
     for head in range(p.heads):
         cols = slice(head * width, (head + 1) * width)
@@ -130,6 +136,9 @@
         return remote(st_out.at[device], st_in.at[me], st_send.at[device], st_recv.at[me], (image, device))
 
     targets(0, lambda device, head: copy_qk(0)(device, head).start())
+
+    loads["o"].wait()
+    loads["og"].wait()
 
     def copy_io(step):
         return remote(
@@ -190,7 +199,7 @@
     ]
     io_in[slot] = o_ref[...]
 
-    load_w.wait()
+    loads["w"].wait()
 
     @pl.loop(0, p.feature // 256)
     def _(step):
@@ -214,13 +223,15 @@
 
     gathered = jnp.concatenate([gv_out[head, :, 0:width] for head in range(p.heads)], axis=1)
     dots_s[...] = row_dots(gathered, o_ref[...])
+    loads["v"].wait()
+    loads["ls"].wait()
     for head in range(p.heads):
         gv_out[head, :, width:depth] = v_ref[:, head * width : (head + 1) * width]
     st_out[...] = jnp.zeros_like(st_out)
     for device in range(peers):
         for j in range(p.first(device + 1) - p.first(device)):
             head = p.first(device) + j
-            st_out[device, 2 * j : 2 * j + 1, :] = -ls_ref[head : head + 1, :]
+            st_out[device, 2 * j : 2 * j + 1, :] = -ls_ref[head]
             st_out[device, 2 * j + 1 : 2 * j + 2, :] = -dots_s[head : head + 1, :]
 
     @pl.loop(0, peers)
@@ -236,8 +247,8 @@
         targets(j, lambda device, head: copy_qk(j)(device, head).start())
         targets(j, lambda device, head: copy_gv(j)(device, head).start())
 
-    for load in loads:
-        load.wait()
+    for name in names[7:]:
+        loads[name].wait()
     tdots_s[...] = row_dots(txt_s[3], txt_s[4])
     st_text[...] = jnp.zeros_like(st_text)
     text_at = slice(p.tokens, p.tokens + p.text_rows)
@@ -259,7 +270,7 @@
         x_gv[j, pad_at] = jnp.zeros((p.total - pad_at.start, depth), BF)
         x_qk[j, text_at] = jnp.concatenate([text_cols(0) * jnp.asarray(scaling, BF), text_cols(1)], axis=1)
         x_gv[j, text_at] = jnp.concatenate([text_cols(3), text_cols(2)], axis=1)
-        st_text[pl.ds(2 * j, 1), 0 : p.text_rows] = -tls_ref[pl.ds(head, 1), :]
+        st_text[pl.ds(2 * j, 1), 0 : p.text_rows] = -tls_ref[head]
         st_text[pl.ds(2 * j + 1, 1), 0 : p.text_rows] = -tdots_s[pl.ds(head, 1), :]
 
     def stats_tile(value):
@@ -299,21 +310,94 @@
 
     far = pl.ds(0, (peers - 1) * rows)
 
-    def text_copy(head, way, device):
-        return remote(
-            tback_ref.at[head], tback_ref.at[head], text_send.at[head, way], text_recv.at[head], (image, device)
-        )
-
-    def send_text(head, upward, downward):
+    def text_copy(source, head, way, device):
+        return remote(source, tback_ref.at[head], text_send.at[head, way], text_recv.at[head], (image, device))
+
+    def send_text(source, head, upward, downward):
         @pl.when(upward & (chip + 1 < chips))
         def _():
-            text_copy(head, 0, me + 2).start()
+            text_copy(source, head, 0, me + 2).start()
 
         @pl.when(downward & (chip > 0))
         def _():
-            text_copy(head, 1, me - 2).start()
-
-        text_copy(head, 2, chip * 2 + 1 - core).start()
+            text_copy(source, head, 1, me - 2).start()
+
+        text_copy(source, head, 2, chip * 2 + 1 - core).start()
+
+    def own_back(j):
+        return pltpu.make_async_copy(result_s.at[j, me], back_ref.at[first + j], own_sem.at[0, j])
+
+    def send_back(j):
+        own_back(j).start()
+
+        @pl.loop(0, peers)
+        def _(step):
+            block = (me + peers // 2 + step) % peers
+
+            @pl.when(block != me)
+            def _():
+                remote(
+                    result_s.at[j, block], back_ref.at[first + j], back_send.at[j, block],
+                    back_recv.at[first + j], (image, block),
+                ).start()
+
+    def own_text(j):
+        return pltpu.make_async_copy(text_s.at[j], tback_ref.at[first + j], own_sem.at[1, j])
+
+    half_chips = chips // 2
+    side, seat = chip // half_chips, chip % half_chips
+    gate = half_chips - 1 + side
+    near, beyond = side * half_chips, (1 - side) * half_chips
+    edge = chip != gate
+
+    def send_sum(number, target, recv, device):
+        remote(
+            sums_out.at[number], target, sums_send.at[number], recv, (image, device * 2 + core)
+        ).start()
+
+    def send_terms():
+        for number in range(half_chips):
+            @pl.when(edge)
+            def _():
+                send_sum(beyond + number, gate_in.at[seat, number], gate_recv.at[seat, number], gate)
+
+        for number in range(half_chips):
+            @pl.when(number != seat)
+            def _():
+                send_sum(near + number, sums_in.at[seat], sums_recv.at[seat], near + number)
+
+    def pass_sums():
+        @pl.when(chip == gate)
+        def _():
+            for number in range(half_chips):
+                @pl.loop(1, half_chips)
+                def _(step):
+                    source = (seat + step) % half_chips
+                    piece = gate_in.at[source, number]
+                    pltpu.make_async_copy(piece, piece, gate_recv.at[source, number]).wait()
+
+                    @pl.loop(0, p.feature // 256)
+                    def _(step):
+                        lanes = pl.ds(pl.multiple_of(step * 256, 256), 256)
+                        total = sums_out[beyond + number, :, lanes].astype(F32)
+                        total += gate_in[source, number, :, lanes].astype(F32)
+                        sums_out[beyond + number, :, lanes] = total.astype(BF)
+
+                send_sum(beyond + number, sums_in.at[half_chips], sums_recv.at[half_chips], beyond + number)
+
+    def pass_text(hop, low, high):
+        for upward in (True, False):
+            source = chip - hop if upward else chip + hop
+
+            @pl.when((source >= 0) & (source < chips))
+            def _():
+                owner = source * 2 + core
+                start, stop = p.first(owner), p.first(owner + 1)
+
+                @pl.loop(start + low, jnp.minimum(stop, start + high))
+                def _(head):
+                    pltpu.make_async_copy(tback_ref.at[head], tback_ref.at[head], text_recv.at[head]).wait()
+                    send_text(tback_ref.at[head], head, upward, not upward)
 
     @pl.loop(0, count)
     def _(j):
@@ -340,38 +424,17 @@
             dk_s[at, :] = jnp.dot(low, q_s[...], preferred_element_type=F32).astype(BF)
             dq_s[...] += lax.dot_general(keys, low, TN, preferred_element_type=F32)
 
-        @pl.loop(0, peers)
-        def _(block):
-            base = pl.multiple_of(block * rows, rows)
-            dq = (dq_s[:, pl.ds(base, rows)].T * scaling).astype(BF)
-            top = jnp.concatenate([dq[:, :width], dk_s[pl.ds(base, rows), :width]], axis=1)
-            dv = dv_s[pl.ds(base, rows), :width]
-            bottom = jnp.concatenate([dv[: rows // 2], dv[rows // 2 :]], axis=1)
-            result_s[j, block, 0:rows] = top
-            result_s[j, block, rows : p.out_rows] = bottom
-
-            @pl.when(block == me)
-            def _():
-                back_ref[head, 0:rows] = top
-                back_ref[head, rows : p.out_rows] = bottom
-
-            @pl.when(block != me)
-            def _():
-                remote(
-                    result_s.at[j, block], back_ref.at[head], back_send.at[j, block], back_recv.at[head],
-                    (image, block),
-                ).start()
-
         dq = (dq_s[:, p.tokens : p.total].T * scaling).astype(BF)
         even, half = p.text_even, p.text_half
-        tback_ref[head, 0:even] = jnp.concatenate(
+        text_s[j, 0:even] = jnp.concatenate(
             [dq[:even, :width], dk_s[p.tokens : p.tokens + even, :width]], axis=1
         )
-        tback_ref[head, even : even + half] = jnp.concatenate(
+        text_s[j, even : even + half] = jnp.concatenate(
             [dv_s[p.tokens : p.tokens + half, :width], dv_s[p.tokens + half : p.tokens + 2 * half, :width]],
             axis=1,
         )
-        send_text(head, True, True)
+        own_text(j).start()
+        send_text(text_s.at[j], head, True, True)
 
         @pl.when(j == 0)
         def _():
@@ -381,7 +444,7 @@
                 pltpu.make_async_copy(io_in.at[source], io_in.at[source], io_recv.at[source]).wait()
                 share_io(step).start()
 
-        @pl.when(j == jnp.minimum(1, count - 1))
+        @pl.when(j == 0)
         def _():
             @pl.loop(0, images)
             def _(index):
@@ -407,54 +470,70 @@
                         )
                     sums_out[number, :, lanes] = total.astype(BF)
 
-            @pl.loop(0, chips)
-            def _(number):
-                @pl.when(number != chip)
-                def _():
-                    remote(
-                        sums_out.at[number], sums_in.at[chip], sums_send.at[number], sums_recv.at[chip],
-                        (image, number * 2 + core),
-                    ).start()
-
-            sums_in[chip] = sums_out[chip]
-
-    @pl.loop(1, chips)
-    def _(hop):
-        for upward in (True, False):
-            source = chip - hop if upward else chip + hop
-
-            @pl.when((source >= 0) & (source < chips))
-            def _():
-                owner = source * 2 + core
-                start = p.first(owner)
-
-                @pl.loop(start, p.first(owner + 1))
-                def _(head):
-                    pltpu.make_async_copy(tback_ref.at[head], tback_ref.at[head], text_recv.at[head]).wait()
-                    send_text(head, upward, not upward)
-
-    @pl.loop(1, chips)
-    def _(step):
-        source = (chip + step) % chips
-        pltpu.make_async_copy(sums_in.at[source], sums_in.at[source], sums_recv.at[source]).wait()
-
-    @pl.loop(0, p.feature // 256)
-    def _(step):
-        lanes = pl.ds(pl.multiple_of(step * 256, 256), 256)
-        total = sums_in[0, :, lanes].astype(F32)
-        for source in range(1, chips):
-            total += sums_in[source, :, lanes].astype(F32)
-        parts_ref[image, :, lanes] = total.astype(BF)
+            send_terms()
+
+        @pl.loop(0, peers)
+        def _(block):
+            base = pl.multiple_of(block * rows, rows)
+            dq = (dq_s[:, pl.ds(base, rows)].T * scaling).astype(BF)
+            top = jnp.concatenate([dq[:, :width], dk_s[pl.ds(base, rows), :width]], axis=1)
+            dv = dv_s[pl.ds(base, rows), :width]
+            bottom = jnp.concatenate([dv[: rows // 2], dv[rows // 2 :]], axis=1)
+            result_s[j, block, 0:rows] = top
+            result_s[j, block, rows : p.out_rows] = bottom
+
+        @pl.when(j == 0)
+        def _():
+            pass_text(1, 0, 1)
+
+        @pl.when(j == jnp.minimum(1, count - 1))
+        def _():
+            pass_sums()
+
+        late = jnp.where(edge, 1, 0)
+
+        @pl.when(j >= late)
+        def _():
+            send_back(j - late)
+
+
+    pass_text(1, 1, p.most)
+
+    @pl.when(edge)
+    def _():
+        send_back(count - 1)
+
+    @pl.loop(0, half_chips + 1)
+    def _(source):
+        @pl.when(source != seat)
+        def _():
+            pltpu.make_async_copy(sums_in.at[source], sums_in.at[source], sums_recv.at[source]).wait()
+
+    @pl.loop(0, half_chips + 1)
+    def _(source):
+        @pl.when(source != seat)
+        def _():
+            @pl.loop(0, p.feature // 256)
+            def _(step):
+                lanes = pl.ds(pl.multiple_of(step * 256, 256), 256)
+                total = sums_out[chip, :, lanes].astype(F32) + sums_in[source, :, lanes].astype(F32)
+                sums_out[chip, :, lanes] = total.astype(BF)
+
+    own_parts = pltpu.make_async_copy(sums_out.at[chip], parts_ref.at[image], own_sem.at[0, p.most])
+    own_parts.start()
 
     def copy_parts(step):
         return remote(
-            parts_ref.at[image], parts_ref.at[image], parts_send.at[step], parts_recv.at[image],
+            sums_out.at[chip], parts_ref.at[image], parts_send.at[step], parts_recv.at[image],
             ((image + step) % images, me),
         )
 
     @pl.loop(1, images)
     def _(step):
         copy_parts(step).start()
+
+    for hop in range(2, chips):
+        pass_text(hop, 0, p.most)
 
     @pl.loop(0, p.heads)
     def _(head):
@@ -478,13 +557,13 @@
         def _(head):
             @pl.when((number <= chip) & (chip + 1 < chips))
             def _():
-                text_copy(head, 0, me).wait_send()
+                text_copy(tback_ref.at[head], head, 0, me).wait_send()
 
             @pl.when((number >= chip) & (chip > 0))
             def _():
-                text_copy(head, 1, me).wait_send()
-
-            text_copy(head, 2, me).wait_send()
+                text_copy(tback_ref.at[head], head, 1, me).wait_send()
+
+            text_copy(tback_ref.at[head], head, 2, me).wait_send()
 
         @pl.when(number != chip)
         def _():
@@ -500,6 +579,13 @@
             def _(j):
                 piece = result_s.at[j, device]
                 pltpu.make_async_copy(piece, piece, back_send.at[j, device]).wait()
+
+    own_parts.wait()
+
+    @pl.loop(0, count)
+    def _(j):
+        own_back(j).wait()
+        own_text(j).wait()
 
     copy_own.wait_send()
     for side in range(2):
@@ -521,7 +607,6 @@
 def exchange(plan, *arrays):
     p = plan
     dma = pltpu.SemaphoreType.DMA
-    vmem = pl.BlockSpec(memory_space=pltpu.VMEM)
     anywhere = pl.BlockSpec(memory_space=pl.ANY)
     pick = up(p.heads, 8)
     wide = (p.total, p.depth)
@@ -532,9 +617,14 @@
             jax.ShapeDtypeStruct((p.heads, p.out_text, p.depth), BF),
             jax.ShapeDtypeStruct((p.images, p.part, p.feature), BF),
         ),
-        in_specs=[vmem] * 6 + [anywhere] * 5 + [vmem, anywhere],
-        out_specs=(vmem,) * 3,
-        scratch_shapes=[
+        in_specs=[anywhere] * 13,
+        out_specs=(anywhere,) * 3,
+        scratch_shapes=[pltpu.VMEM((p.rows, p.feature), BF)] * 4
+        + [
+            pltpu.VMEM((p.rows, p.model), BF),
+            pltpu.VMEM((p.heads, 1, p.rows), F32),
+            pltpu.VMEM((p.heads, 1, p.text_rows), F32),
+            pltpu.VMEM((p.most, p.out_text, p.depth), BF),
             pltpu.VMEM((p.model, p.feature), BF),
             pltpu.VMEM((5, p.text_rows, p.feature), BF),
             pltpu.VMEM((p.heads, p.rows, p.depth), BF),
@@ -556,8 +646,9 @@
             pltpu.VMEM((p.chips, p.part, 2 * p.images * p.rows), BF),
             pltpu.VMEM((2 * p.images, p.rows, p.feature), BF),
             pltpu.VMEM((p.chips, p.part, p.feature), BF),
-            pltpu.VMEM((p.chips, p.part, p.feature), BF),
-            dma((6,)),
+            pltpu.VMEM((p.chips // 2 + 1, p.part, p.feature), BF),
+            pltpu.VMEM((p.chips // 2, p.chips // 2, p.part, p.feature), BF),
+            dma((13,)), dma((2, p.most + 1)),
             dma((p.heads,)), dma((p.most,)),
             dma((p.heads,)), dma((p.most,)),
             dma((p.peers,)), dma((p.peers,)),
@@ -565,7 +656,7 @@
             dma((p.heads, 3)), dma((p.heads,)),
             dma((2 * p.images,)), dma((2 * p.images,)),
             dma((p.images, 2)), dma((2 * p.images,)),
-            dma((p.chips,)), dma((p.chips,)),
+            dma((p.chips,)), dma((p.chips // 2 + 1,)), dma((p.chips // 2, p.chips // 2)),
             dma((p.images,)), dma((p.images,)),
         ],
         compiler_params=pltpu.CompilerParams(
@@ -574,41 +665,84 @@
     )(*arrays)
 
 
-def finish_kernel(plan, back_ref, tback_ref, parts_ref, dq_ref, dk_ref, dv_ref, tdq_ref, tdk_ref, tdv_ref, wg_ref):
+def finish_kernel(
+    plan, back_in, tback_in, parts_in, dq_out, dk_out, dv_out, tdq_out, tdk_out, tdv_out, wg_out,
+    back_ref, tback_ref, parts_ref, dq_ref, dk_ref, dv_ref, tdq_ref, tdk_ref, tdv_ref, wg_ref,
+    load_sem, store_sem,
+):
     p = plan
     width, rows, half, even = p.width, p.rows, p.text_half, p.text_even
-    for pair in range(p.heads // 2):
-        lanes = slice(pair * p.depth, (pair + 1) * p.depth)
-
-        def join(ref, at, cols):
-            return jnp.concatenate([ref[2 * pair, at, cols], ref[2 * pair + 1, at, cols]], axis=1)
-
-        left, right = slice(0, width), slice(width, p.depth)
-        dq_ref[:, lanes] = join(back_ref, slice(0, rows), left)
-        dk_ref[:, lanes] = join(back_ref, slice(0, rows), right)
-        dv_ref[0 : rows // 2, lanes] = join(back_ref, slice(rows, p.out_rows), left)
-        dv_ref[rows // 2 : rows, lanes] = join(back_ref, slice(rows, p.out_rows), right)
-        tdq_ref[:, lanes] = join(tback_ref, slice(0, p.text_rows), left)
-        tdk_ref[:, lanes] = join(tback_ref, slice(0, p.text_rows), right)
-        tdv_ref[0:half, lanes] = join(tback_ref, slice(even, even + half), left)
-        tdv_ref[half : p.text_rows, lanes] = join(tback_ref, slice(even, even + p.text_rows - half), right)
+    group = p.heads // p.finish_steps
+    text_loads = [
+        pltpu.make_async_copy(
+            tback_in.at[pl.ds(step * group, group)], tback_ref.at[pl.ds(step * group, group)], load_sem.at[2 + step]
+        )
+        for step in range(p.finish_steps)
+    ]
+    load_parts = pltpu.make_async_copy(parts_in, parts_ref, load_sem.at[0])
+    load_back = pltpu.make_async_copy(back_in, back_ref, load_sem.at[1])
+    for load in (load_parts, load_back, *text_loads):
+        load.start()
+    stores = []
+
+    def store(source, target):
+        copy = pltpu.make_async_copy(source, target, store_sem.at[len(stores)])
+        copy.start()
+        stores.append(copy)
+
+    load_parts.wait()
     for number in range(p.images):
         start = p.part_start(number)
         stop = min(start + p.part, p.share)
         wg_ref[start:stop, :] = parts_ref[number, 0 : stop - start, :].astype(F32)
+    store(wg_ref, wg_out)
+
+    def join(ref, pair, at, cols):
+        return jnp.concatenate([ref[2 * pair, at, cols], ref[2 * pair + 1, at, cols]], axis=1)
+
+    left, right = slice(0, width), slice(width, p.depth)
+    load_back.wait()
+    for pair in range(p.heads // 2):
+        lanes = slice(pair * p.depth, (pair + 1) * p.depth)
+        dq_ref[:, lanes] = join(back_ref, pair, slice(0, rows), left)
+        dk_ref[:, lanes] = join(back_ref, pair, slice(0, rows), right)
+        dv_ref[0 : rows // 2, lanes] = join(back_ref, pair, slice(rows, p.out_rows), left)
+        dv_ref[rows // 2 : rows, lanes] = join(back_ref, pair, slice(rows, p.out_rows), right)
+    store(dq_ref, dq_out)
+    store(dk_ref, dk_out)
+    store(dv_ref, dv_out)
+    for step in range(p.finish_steps):
+        text_loads[step].wait()
+        for pair in range(step * group // 2, (step + 1) * group // 2):
+            lanes = slice(pair * p.depth, (pair + 1) * p.depth)
+            tdq_ref[:, lanes] = join(tback_ref, pair, slice(0, p.text_rows), left)
+            tdk_ref[:, lanes] = join(tback_ref, pair, slice(0, p.text_rows), right)
+            tdv_ref[0:half, lanes] = join(tback_ref, pair, slice(even, even + half), left)
+            tdv_ref[half : p.text_rows, lanes] = join(tback_ref, pair, slice(even, even + p.text_rows - half), right)
+        lanes = slice(step * group * width, (step + 1) * group * width)
+        for source, target in ((tdq_ref, tdq_out), (tdk_ref, tdk_out), (tdv_ref, tdv_out)):
+            store(source.at[:, lanes], target.at[:, lanes])
+    for copy in stores:
+        copy.wait()
 
 
 def finish(plan, back, tback, parts):
     p = plan
-    vmem = pl.BlockSpec(memory_space=pltpu.VMEM)
+    anywhere = pl.BlockSpec(memory_space=pl.ANY)
     token = jax.ShapeDtypeStruct((p.rows, p.feature), BF)
     text = jax.ShapeDtypeStruct((p.text_rows, p.feature), BF)
+    outs = (token,) * 3 + (text,) * 3 + (jax.ShapeDtypeStruct((p.share, p.feature), F32),)
     return pl.pallas_call(
         functools.partial(finish_kernel, p),
-        out_shape=(token,) * 3 + (text,) * 3 + (jax.ShapeDtypeStruct((p.share, p.feature), F32),),
-        in_specs=[vmem] * 3,
-        out_specs=(vmem,) * 7,
-        compiler_params=pltpu.CompilerParams(vmem_limit_bytes=40 << 20),
+        out_shape=outs,
+        in_specs=[anywhere] * 3,
+        out_specs=(anywhere,) * 7,
+        scratch_shapes=[pltpu.VMEM(value.shape, value.dtype) for value in (back, tback, parts, *outs)]
+        + [
+            pltpu.SemaphoreType.DMA((2 + p.finish_steps,)),
+            pltpu.SemaphoreType.DMA((4 + 3 * p.finish_steps,)),
+        ],
+        compiler_params=pltpu.CompilerParams(vmem_limit_bytes=60 << 20),
     )(back, tback, parts)
 
 
@@ -638,8 +772,8 @@
     )
     results = exchange(
         plan,
-        image_query[0], image_key[0], image_value[0], image_output[0], output_grad[0], image_logsum[0].T,
-        text_query[0], text_key[0], text_value[0], text_output[0], text_grad[0], text_logsum[0].T,
+        image_query[0], image_key[0], image_value[0], image_output[0], output_grad[0], image_logsum.transpose(2, 0, 1),
+        text_query[0], text_key[0], text_value[0], text_output[0], text_grad[0], text_logsum.transpose(2, 0, 1),
         out_weight,
     )
     *grads, weight_grad = finish(plan, *results)

time: 116 us -> 93.2 us (0.80)
  Pallas kernels: 109 us -> 92.1 us
  local copies, waits for them, and re-layouts: 6.75 us -> 0 us
    pallas_call x1, Pallas kernels: 105 us -> 88.4 us  [exchange(): pl.pallas_call(functools.partial(exchange_kernel, p), out_shape=(jax.Shap...]
    unnamed x8 -> x0, local copies, waits for them, and re-layouts: 6.75 us -> none
where the time goes in v1:
time: 93.2 us; the launch traced here: 92.8 us
  Pallas kernels  92.1 us (99%)
    pallas_call x1, Pallas kernels, exchange(): pl.pallas_call(functools.partial(exchange_kernel, p), out_shape=(jax.Shap...  88.4 us
    pallas_call x1, Pallas kernels, finish(): pl.pallas_call(functools.partial(finish_kernel, p), out_shape=outs, in_sp...  3.75 us

profile of v1, /device:TPU:1, one launch (start us, length us, event | category | flops | bytes accessed | tf_op | source)
XLA Modules:
  0.0 92.8 jit_solution(16943214133095142807)
XLA Ops:
  0.6 88.4 %shard_map.180 = (bf16[20,192,128]{2,1,0:T(8,128)(2,1)}, bf16[20,512,128]{2,1,0:T(8,128)(2,1)}, bf16[4,80,1280]{2,1,0:T(8,128)(2,1)}) custom-call(bf16[128,1280]{1,0:T(8,128)(2,1)} %bitcast.24, bf16[128,1280]{1,0:T(8,128)(2,1)} %bitcast.25, bf16[128,1280]{1,0:T(8,128)(2,1)} %bitcast.26, bf16[128,1280]{1,0:T(8,128)(2,1)} %bitcast.27, ...), custom_call_target="tpu_custom_call" | custom-call | tf_op jit(solution)/shard_map/pallas_call | solution.py:613
  89.0 3.8 %shard_map.181 = (bf16[128,1280]{1,0:T(8,128)(2,1)}, bf16[128,1280]{1,0:T(8,128)(2,1)}, bf16[128,1280]{1,0:T(8,128)(2,1)}, bf16[333,1280]{1,0:T(8,128)(2,1)}, bf...) custom-call(bf16[20,192,128]{2,1,0:T(8,128)(2,1)} %get-tuple-element.17.back_in, ...), custom_call_target="tpu_custom_call" | custom-call | tf_op jit(solution)/shard_map/pallas_call | solution.py:735

commit v2 on v1

--- a/solution.py
+++ b/solution.py
@@ -56,9 +56,9 @@
     q_in, k_in, v_in, o_in, og_in_ref, ls_in,
     tq_ref, tk_ref, tv_ref, to_ref, tg_ref, tls_in, w_ref,
     back_ref, tback_ref, parts_ref,
-    q_ref, k_ref, v_ref, o_ref, og_ref, ls_ref, tls_ref, text_s, w_s, txt_s, qk_out, gv_out, st_out, x_qk, x_gv, st_in, st_text, dots_s, tdots_s, stat_s,
+    q_ref, k_ref, v_ref, o_ref, og_ref, ls_ref, tls_ref, text_s, w_s, txt_s, x_out, st_out, x_in, st_in, st_text, dots_s, tdots_s, stat_s,
     q_s, k_s, v_s, g_s, dk_s, dv_s, dq_s, result_s, ogt_s, og_in, io_in, sums_out, sums_in, gate_in,
-    local_sem, own_sem, qk_send, qk_recv, gv_send, gv_recv, st_send, st_recv, back_send, back_recv,
+    local_sem, own_sem, x_send, x_recv, st_send, st_recv, back_send, back_recv,
     text_send, text_recv, io_send, io_recv, og_send, og_recv, sums_send, sums_recv, gate_recv,
     parts_send, parts_recv,
 ):
@@ -92,23 +92,26 @@
                 barrier, inc=1, device_id=((image + step) % images, chip * 2 + side), device_id_type=MESH
             )
 
-    names = ("q", "k", "o", "og", "w", "v", "ls", "tq", "tk", "tv", "tg", "to", "tls")
-    pairs = (
-        (q_in, q_ref), (k_in, k_ref), (o_in, o_ref), (og_in_ref, og_ref), (w_ref, w_s), (v_in, v_ref), (ls_in, ls_ref),
-        (tq_ref, txt_s.at[0]), (tk_ref, txt_s.at[1]), (tv_ref, txt_s.at[2]), (tg_ref, txt_s.at[3]),
-        (to_ref, txt_s.at[4]), (tls_in, tls_ref),
-    )
+    pairs = {
+        "q": (q_in, q_ref), "k": (k_in, k_ref), "o": (o_in, o_ref), "og": (og_in_ref, og_ref), "w": (w_ref, w_s),
+        "v": (v_in, v_ref), "ls": (ls_in, ls_ref), "tls": (tls_in, tls_ref),
+    }
     loads = {}
-    for number, (name, (source, target)) in enumerate(zip(names, pairs)):
+    for number, (name, (source, target)) in enumerate(pairs.items()):
         loads[name] = pltpu.make_async_copy(source, target, local_sem.at[number])
         loads[name].start()
+    for number, source in enumerate((tq_ref, tk_ref, tv_ref, tg_ref, to_ref)):
+        pltpu.make_async_copy(source, txt_s.at[number], local_sem.at[len(pairs)]).start()
+
+    def wait_bytes(ref, sem):
+        pltpu.make_async_copy(ref, ref, sem).wait()
 
     loads["q"].wait()
     loads["k"].wait()
 
     for head in range(p.heads):
         cols = slice(head * width, (head + 1) * width)
-        qk_out[head] = jnp.concatenate([q_ref[:, cols] * jnp.asarray(scaling, BF), k_ref[:, cols]], axis=1)
+        x_out[head, 0] = jnp.concatenate([q_ref[:, cols] * jnp.asarray(scaling, BF), k_ref[:, cols]], axis=1)
 
     pl.semaphore_wait(barrier, peers - 1 + 2 * (images - 1))
 
@@ -122,38 +125,37 @@
             def _():
                 action(device, head)
 
-    def copy_qk(j):
+    def copy_x(j, part):
+        if j == 0:
+            return lambda device, head: remote(
+                x_out.at[head, part], x_in.at[j, part, my_rows], x_send.at[part], x_recv.at[part], (image, device)
+            )
         return lambda device, head: remote(
-            qk_out.at[head], x_qk.at[j, my_rows], qk_send.at[head], qk_recv.at[j], (image, device)
-        )
-
-    def copy_gv(j):
-        return lambda device, head: remote(
-            gv_out.at[head], x_gv.at[j, my_rows], gv_send.at[head], gv_recv.at[j], (image, device)
+            x_out.at[head], x_in.at[j, :, my_rows], x_send.at[2], x_recv.at[1 + j], (image, device)
         )
 
     def copy_st(device):
-        return remote(st_out.at[device], st_in.at[me], st_send.at[device], st_recv.at[me], (image, device))
-
-    targets(0, lambda device, head: copy_qk(0)(device, head).start())
+        return remote(st_out.at[device], st_in.at[me], st_send.at[0], st_recv.at[0], (image, device))
+
+    targets(0, lambda device, head: copy_x(0, 0)(device, head).start())
 
     loads["o"].wait()
     loads["og"].wait()
 
     def copy_io(step):
         return remote(
-            o_ref, io_in.at[slot], io_send.at[step], io_recv.at[slot], ((image + step) % images, me)
+            o_ref, io_in.at[slot], io_send.at[0], io_recv.at[0], ((image + step) % images, me)
         )
 
     def share_io(step):
         source = ((image + step) % images) * 2 + core
         return remote(
-            io_in.at[source], io_in.at[source], io_send.at[images + step], io_recv.at[source],
+            io_in.at[source], io_in.at[source], io_send.at[0], io_recv.at[1],
             (image, chip * 2 + 1 - core),
         )
 
     copy_own = remote(
-        o_ref, io_in.at[slot], io_send.at[0], io_recv.at[slot], (image, chip * 2 + 1 - core)
+        o_ref, io_in.at[slot], io_send.at[0], io_recv.at[1], (image, chip * 2 + 1 - core)
     )
 
     @pl.loop(1, images)
@@ -179,8 +181,8 @@
         return remote(
             ogt_s.at[side, :, pl.ds(p.part_start(other), p.part)],
             og_in.at[:, :, pl.ds(pl.multiple_of(slot * rows, rows), rows)],
-            og_send.at[step, side],
-            og_recv.at[slot],
+            og_send.at[0],
+            og_recv.at[0],
             (other, chip * 2 + side),
         )
 
@@ -208,7 +210,7 @@
         per = 256 // width
         for number in range(per):
             head = step * per + number
-            gv_out[head, :, 0:width] = g_cols[:, number * width : (number + 1) * width]
+            x_out[head, 1, :, 0:width] = g_cols[:, number * width : (number + 1) * width]
 
     pick_rows = up(p.heads, 8)
     tag = lax.broadcasted_iota(jnp.int32, (pick_rows, p.feature), 0)
@@ -221,12 +223,12 @@
             picker, product, NT, precision=lax.Precision.HIGHEST, preferred_element_type=F32
         )
 
-    gathered = jnp.concatenate([gv_out[head, :, 0:width] for head in range(p.heads)], axis=1)
+    gathered = jnp.concatenate([x_out[head, 1, :, 0:width] for head in range(p.heads)], axis=1)
     dots_s[...] = row_dots(gathered, o_ref[...])
     loads["v"].wait()
     loads["ls"].wait()
     for head in range(p.heads):
-        gv_out[head, :, width:depth] = v_ref[:, head * width : (head + 1) * width]
+        x_out[head, 1, :, width:depth] = v_ref[:, head * width : (head + 1) * width]
     st_out[...] = jnp.zeros_like(st_out)
     for device in range(peers):
         for j in range(p.first(device + 1) - p.first(device)):
@@ -242,13 +244,12 @@
         def _():
             copy_st(device).start()
 
-    targets(0, lambda device, head: copy_gv(0)(device, head).start())
+    targets(0, lambda device, head: copy_x(0, 1)(device, head).start())
     for j in range(1, p.most):
-        targets(j, lambda device, head: copy_qk(j)(device, head).start())
-        targets(j, lambda device, head: copy_gv(j)(device, head).start())
-
-    for name in names[7:]:
-        loads[name].wait()
+        targets(j, lambda device, head: copy_x(j, 0)(device, head).start())
+
+    loads["tls"].wait()
+    wait_bytes(txt_s, local_sem.at[len(pairs)])
     tdots_s[...] = row_dots(txt_s[3], txt_s[4])
     st_text[...] = jnp.zeros_like(st_text)
     text_at = slice(p.tokens, p.tokens + p.text_rows)
@@ -264,12 +265,12 @@
             value = txt_s[number, :, tile]
             return jnp.where(odd, value[:, width:], value[:, :width])
 
-        x_qk[j, my_rows] = qk_out[head]
-        x_gv[j, my_rows] = gv_out[head]
-        x_qk[j, pad_at] = jnp.zeros((p.total - pad_at.start, depth), BF)
-        x_gv[j, pad_at] = jnp.zeros((p.total - pad_at.start, depth), BF)
-        x_qk[j, text_at] = jnp.concatenate([text_cols(0) * jnp.asarray(scaling, BF), text_cols(1)], axis=1)
-        x_gv[j, text_at] = jnp.concatenate([text_cols(3), text_cols(2)], axis=1)
+        x_in[j, 0, my_rows] = x_out[head, 0]
+        x_in[j, 1, my_rows] = x_out[head, 1]
+        x_in[j, 0, pad_at] = jnp.zeros((p.total - pad_at.start, depth), BF)
+        x_in[j, 1, pad_at] = jnp.zeros((p.total - pad_at.start, depth), BF)
+        x_in[j, 0, text_at] = jnp.concatenate([text_cols(0) * jnp.asarray(scaling, BF), text_cols(1)], axis=1)
+        x_in[j, 1, text_at] = jnp.concatenate([text_cols(3), text_cols(2)], axis=1)
         st_text[pl.ds(2 * j, 1), 0 : p.text_rows] = -tls_ref[head]
         st_text[pl.ds(2 * j + 1, 1), 0 : p.text_rows] = -tdots_s[pl.ds(head, 1), :]
 
@@ -291,10 +292,7 @@
 
     st_in[me] = st_out[me]
 
-    @pl.loop(1, peers)
-    def _(step):
-        source = (me + step) % peers
-        remote(st_out.at[0], st_in.at[source], st_send.at[0], st_recv.at[source], (image, source)).wait_recv()
+    wait_bytes(st_in.at[pl.ds(0, peers - 1)], st_recv.at[0])
 
     @pl.loop(0, peers)
     def _(source):
@@ -310,22 +308,27 @@
 
     far = pl.ds(0, (peers - 1) * rows)
 
-    def text_copy(source, head, way, device):
-        return remote(source, tback_ref.at[head], text_send.at[head, way], text_recv.at[head], (image, device))
-
-    def send_text(source, head, upward, downward):
+    others = chips * p.most
+
+    def text_slot(head, owner):
+        return owner // 2 * p.most + head - p.first(owner)
+
+    def send_text(source, head, owner, upward, downward):
+        def send(way, recv, device):
+            remote(source, tback_ref.at[head], text_send.at[way], text_recv.at[recv], (image, device)).start()
+
         @pl.when(upward & (chip + 1 < chips))
         def _():
-            text_copy(source, head, 0, me + 2).start()
+            send(0, text_slot(head, owner), me + 2)
 
         @pl.when(downward & (chip > 0))
         def _():
-            text_copy(source, head, 1, me - 2).start()
-
-        text_copy(source, head, 2, chip * 2 + 1 - core).start()
+            send(1, text_slot(head, owner), me - 2)
+
+        send(2, others, chip * 2 + 1 - core)
 
     def own_back(j):
-        return pltpu.make_async_copy(result_s.at[j, me], back_ref.at[first + j], own_sem.at[0, j])
+        return pltpu.make_async_copy(result_s.at[j, me], back_ref.at[first + j], own_sem.at[0])
 
     def send_back(j):
         own_back(j).start()
@@ -337,12 +340,12 @@
             @pl.when(block != me)
             def _():
                 remote(
-                    result_s.at[j, block], back_ref.at[first + j], back_send.at[j, block],
-                    back_recv.at[first + j], (image, block),
+                    result_s.at[j, block], back_ref.at[first + j], back_send.at[0], back_recv.at[0],
+                    (image, block),
                 ).start()
 
     def own_text(j):
-        return pltpu.make_async_copy(text_s.at[j], tback_ref.at[first + j], own_sem.at[1, j])
+        return pltpu.make_async_copy(text_s.at[j], tback_ref.at[first + j], own_sem.at[1])
 
     half_chips = chips // 2
     side, seat = chip // half_chips, chip % half_chips
@@ -352,29 +355,29 @@
 
     def send_sum(number, target, recv, device):
         remote(
-            sums_out.at[number], target, sums_send.at[number], recv, (image, device * 2 + core)
+            sums_out.at[number], target, sums_send.at[0], recv, (image, device * 2 + core)
         ).start()
 
     def send_terms():
         for number in range(half_chips):
             @pl.when(edge)
             def _():
-                send_sum(beyond + number, gate_in.at[seat, number], gate_recv.at[seat, number], gate)
+                send_sum(beyond + number, gate_in.at[seat, number], gate_recv.at[0], gate)
 
         for number in range(half_chips):
             @pl.when(number != seat)
             def _():
-                send_sum(near + number, sums_in.at[seat], sums_recv.at[seat], near + number)
+                send_sum(near + number, sums_in.at[seat], sums_recv.at[0], near + number)
 
     def pass_sums():
         @pl.when(chip == gate)
         def _():
+            if half_chips > 1:
+                wait_bytes(gate_in.at[pl.ds(0, half_chips - 1)], gate_recv.at[0])
             for number in range(half_chips):
                 @pl.loop(1, half_chips)
                 def _(step):
                     source = (seat + step) % half_chips
-                    piece = gate_in.at[source, number]
-                    pltpu.make_async_copy(piece, piece, gate_recv.at[source, number]).wait()
 
                     @pl.loop(0, p.feature // 256)
                     def _(step):
@@ -383,31 +386,40 @@
                         total += gate_in[source, number, :, lanes].astype(F32)
                         sums_out[beyond + number, :, lanes] = total.astype(BF)
 
-                send_sum(beyond + number, sums_in.at[half_chips], sums_recv.at[half_chips], beyond + number)
-
-    def pass_text(hop, low, high):
+                send_sum(beyond + number, sums_in.at[half_chips], sums_recv.at[0], beyond + number)
+
+    def pass_text(hop, low, high, inward=(True, False)):
         for upward in (True, False):
             source = chip - hop if upward else chip + hop
-
-            @pl.when((source >= 0) & (source < chips))
+            inner = side == (0 if upward else 1)
+            wanted = {(True,): inner, (False,): ~inner}.get(inward, True)
+
+            @pl.when((source >= 0) & (source < chips) & wanted)
             def _():
                 owner = source * 2 + core
                 start, stop = p.first(owner), p.first(owner + 1)
 
                 @pl.loop(start + low, jnp.minimum(stop, start + high))
                 def _(head):
-                    pltpu.make_async_copy(tback_ref.at[head], tback_ref.at[head], text_recv.at[head]).wait()
-                    send_text(tback_ref.at[head], head, upward, not upward)
+                    wait_bytes(tback_ref.at[head], text_recv.at[text_slot(head, owner)])
+                    send_text(tback_ref.at[head], head, owner, upward, not upward)
 
     @pl.loop(0, count)
     def _(j):
         head = first + j
-        pltpu.make_async_copy(x_qk.at[j, far], x_qk.at[j, far], qk_recv.at[j]).wait()
-        pltpu.make_async_copy(x_gv.at[j, far], x_gv.at[j, far], gv_recv.at[j]).wait()
-        both = x_qk[j]
+        @pl.when(j == 0)
+        def _():
+            for part in range(2):
+                wait_bytes(x_in.at[0, part, far], x_recv.at[part])
+
+        @pl.when(j > 0)
+        def _():
+            wait_bytes(x_in.at[j, :, far], x_recv.at[1 + j])
+
+        both = x_in[j, 0]
         q_s[...] = jnp.where(lane < width, both, stat_s[...])
         k_s[...] = jnp.concatenate([both[:, width:], ones(2 * j)], axis=1)
-        both = x_gv[j]
+        both = x_in[j, 1]
         g_s[...] = jnp.where(lane < width, both, stat_s[...])
         v_s[...] = jnp.concatenate([both[:, width:], ones(2 * j + 1)], axis=1)
         dq_s[...] = jnp.zeros_like(dq_s)
@@ -434,28 +446,21 @@
             axis=1,
         )
         own_text(j).start()
-        send_text(text_s.at[j], head, True, True)
+        send_text(text_s.at[j], head, me, True, True)
 
         @pl.when(j == 0)
         def _():
+            if images > 1:
+                wait_bytes(io_in.at[pl.ds(0, images - 1)], io_recv.at[0])
+
             @pl.loop(1, images)
             def _(step):
-                source = ((image + step) % images) * 2 + core
-                pltpu.make_async_copy(io_in.at[source], io_in.at[source], io_recv.at[source]).wait()
                 share_io(step).start()
 
         @pl.when(j == 0)
         def _():
-            @pl.loop(0, images)
-            def _(index):
-                source = index * 2 + 1 - core
-                pltpu.make_async_copy(io_in.at[source], io_in.at[source], io_recv.at[source]).wait()
-
-            @pl.loop(1, 2 * images)
-            def _(step):
-                source = (slot + step) % (2 * images)
-                piece = og_in.at[:, :, pl.ds(pl.multiple_of(source * rows, rows), rows)]
-                pltpu.make_async_copy(piece, piece, og_recv.at[source]).wait()
+            wait_bytes(io_in.at[pl.ds(0, images)], io_recv.at[1])
+            wait_bytes(og_in.at[:, :, pl.ds(0, (2 * images - 1) * rows)], og_recv.at[0])
 
             @pl.loop(0, p.feature // 256)
             def _(step):
@@ -490,24 +495,23 @@
         def _():
             pass_sums()
 
-        late = jnp.where(edge, 1, 0)
-
-        @pl.when(j >= late)
-        def _():
-            send_back(j - late)
-
-
-    pass_text(1, 1, p.most)
-
-    @pl.when(edge)
-    def _():
-        send_back(count - 1)
-
-    @pl.loop(0, half_chips + 1)
-    def _(source):
-        @pl.when(source != seat)
-        def _():
-            pltpu.make_async_copy(sums_in.at[source], sums_in.at[source], sums_recv.at[source]).wait()
+        @pl.when(j == jnp.where(edge, jnp.minimum(1, count - 1), 0))
+        def _():
+            send_back(0)
+
+
+    pass_text(1, 1, p.most, (True,))
+
+    @pl.loop(1, count)
+    def _(j):
+        send_back(j)
+
+    pass_text(1, 1, 2, (False,))
+    if chips > 2:
+        pass_text(2, 0, 1)
+    pass_text(1, 2, p.most, (False,))
+
+    wait_bytes(sums_in.at[pl.ds(0, half_chips)], sums_recv.at[0])
 
     @pl.loop(0, half_chips + 1)
     def _(source):
@@ -519,12 +523,12 @@
                 total = sums_out[chip, :, lanes].astype(F32) + sums_in[source, :, lanes].astype(F32)
                 sums_out[chip, :, lanes] = total.astype(BF)
 
-    own_parts = pltpu.make_async_copy(sums_out.at[chip], parts_ref.at[image], own_sem.at[0, p.most])
+    own_parts = pltpu.make_async_copy(sums_out.at[chip], parts_ref.at[image], own_sem.at[2])
     own_parts.start()
 
     def copy_parts(step):
         return remote(
-            sums_out.at[chip], parts_ref.at[image], parts_send.at[step], parts_recv.at[image],
+            sums_out.at[chip], parts_ref.at[image], parts_send.at[0], parts_recv.at[0],
             ((image + step) % images, me),
         )
 
@@ -532,76 +536,46 @@
     def _(step):
         copy_parts(step).start()
 
-    for hop in range(2, chips):
+    if chips > 2:
+        pass_text(2, 1, p.most)
+    for hop in range(3, chips):
         pass_text(hop, 0, p.most)
 
-    @pl.loop(0, p.heads)
-    def _(head):
-        @pl.when((head < first) | (head >= first + count))
-        def _():
-            pltpu.make_async_copy(back_ref.at[head], back_ref.at[head], back_recv.at[head]).wait()
-            pltpu.make_async_copy(qk_out.at[head], qk_out.at[head], qk_send.at[head]).wait()
-            pltpu.make_async_copy(gv_out.at[head], gv_out.at[head], gv_send.at[head]).wait()
-
-    @pl.loop(0, chips)
-    def _(number):
-        owner = number * 2 + 1 - core
-
-        @pl.loop(p.first(owner), p.first(owner + 1))
-        def _(head):
-            pltpu.make_async_copy(tback_ref.at[head], tback_ref.at[head], text_recv.at[head]).wait()
-
-        owner = number * 2 + core
-
-        @pl.loop(p.first(owner), p.first(owner + 1))
-        def _(head):
-            @pl.when((number <= chip) & (chip + 1 < chips))
-            def _():
-                text_copy(tback_ref.at[head], head, 0, me).wait_send()
-
-            @pl.when((number >= chip) & (chip > 0))
-            def _():
-                text_copy(tback_ref.at[head], head, 1, me).wait_send()
-
-            text_copy(tback_ref.at[head], head, 2, me).wait_send()
-
-        @pl.when(number != chip)
-        def _():
-            pltpu.make_async_copy(sums_out.at[number], sums_out.at[number], sums_send.at[number]).wait()
-
-    @pl.loop(0, peers)
-    def _(device):
-        @pl.when(device != me)
-        def _():
-            pltpu.make_async_copy(st_out.at[device], st_out.at[device], st_send.at[device]).wait()
-
-            @pl.loop(0, count)
-            def _(j):
-                piece = result_s.at[j, device]
-                pltpu.make_async_copy(piece, piece, back_send.at[j, device]).wait()
-
     own_parts.wait()
-
-    @pl.loop(0, count)
-    def _(j):
-        own_back(j).wait()
-        own_text(j).wait()
-
-    copy_own.wait_send()
-    for side in range(2):
-        @pl.when(core != side)
-        def _():
-            copy_og(0, side).wait_send()
-
-    @pl.loop(1, images)
-    def _(step):
-        copy_io(step).wait_send()
-        share_io(step).wait_send()
-        copy_parts(step).wait_send()
-        for side in range(2):
-            copy_og(step, side).wait_send()
-        source = (image + step) % images
-        pltpu.make_async_copy(parts_ref.at[source], parts_ref.at[source], parts_recv.at[source]).wait()
+    if images > 1:
+        wait_bytes(parts_ref.at[pl.ds(0, images - 1)], parts_recv.at[0])
+        wait_bytes(parts_ref.at[pl.ds(0, images - 1)], parts_send.at[0])
+    wait_bytes(io_in.at[pl.ds(0, 2 * images - 1)], io_send.at[0])
+    wait_bytes(og_in.at[:, :, pl.ds(0, (2 * images - 1) * rows)], og_send.at[0])
+    wait_bytes(st_in.at[pl.ds(0, peers - 1)], st_send.at[0])
+    if chips > 1:
+        wait_bytes(sums_out.at[pl.ds(0, chips - 1)], sums_send.at[0])
+
+    def heads_of(number, side):
+        return p.first(number * 2 + side + 1) - p.first(number * 2 + side)
+
+    for device in range(peers):
+        here, at = device // 2, device % 2
+        mine = heads_of(here, at)
+        same = [heads_of(number, at) for number in range(chips)]
+        upward = sum(same[: here + 1]) if here + 1 < chips else 0
+        downward = sum(same[here:]) if here > 0 else 0
+        partner = p.heads - sum(same)
+
+        @pl.when(me == device)
+        def _():
+            wait_bytes(back_ref.at[pl.ds(0, mine)], own_sem.at[0])
+            wait_bytes(tback_ref.at[pl.ds(0, mine)], own_sem.at[1])
+            for part in range(2):
+                wait_bytes(x_out.at[pl.ds(0, peers - 1), part], x_send.at[part])
+            if p.heads - peers > mine - 1:
+                wait_bytes(x_out.at[pl.ds(0, p.heads - peers - mine + 1)], x_send.at[2])
+            wait_bytes(result_s.at[pl.ds(0, mine), pl.ds(0, peers - 1)], back_send.at[0])
+            wait_bytes(back_ref.at[pl.ds(0, p.heads - mine)], back_recv.at[0])
+            for way, blocks in enumerate((upward, downward, sum(same))):
+                if blocks:
+                    wait_bytes(tback_ref.at[pl.ds(0, blocks)], text_send.at[way])
+            wait_bytes(tback_ref.at[pl.ds(0, partner)], text_recv.at[others])
 
 
 def exchange(plan, *arrays):
@@ -627,11 +601,9 @@
             pltpu.VMEM((p.most, p.out_text, p.depth), BF),
             pltpu.VMEM((p.model, p.feature), BF),
             pltpu.VMEM((5, p.text_rows, p.feature), BF),
-            pltpu.VMEM((p.heads, p.rows, p.depth), BF),
-            pltpu.VMEM((p.heads, p.rows, p.depth), BF),
+            pltpu.VMEM((p.heads, 2, p.rows, p.depth), BF),
             pltpu.VMEM((p.peers, p.stat_rows, p.rows), F32),
-            pltpu.VMEM((p.most, *wide), BF),
-            pltpu.VMEM((p.most, *wide), BF),
+            pltpu.VMEM((p.most, 2, *wide), BF),
             pltpu.VMEM((p.peers, p.stat_rows, p.rows), F32),
             pltpu.VMEM((p.stat_rows, p.total - p.tokens), F32),
             pltpu.VMEM((pick, p.rows), F32),
@@ -648,16 +620,15 @@
             pltpu.VMEM((p.chips, p.part, p.feature), BF),
             pltpu.VMEM((p.chips // 2 + 1, p.part, p.feature), BF),
             pltpu.VMEM((p.chips // 2, p.chips // 2, p.part, p.feature), BF),
-            dma((13,)), dma((2, p.most + 1)),
-            dma((p.heads,)), dma((p.most,)),
-            dma((p.heads,)), dma((p.most,)),
-            dma((p.peers,)), dma((p.peers,)),
-            dma((p.most, p.peers)), dma((p.heads,)),
-            dma((p.heads, 3)), dma((p.heads,)),
-            dma((2 * p.images,)), dma((2 * p.images,)),
-            dma((p.images, 2)), dma((2 * p.images,)),
-            dma((p.chips,)), dma((p.chips // 2 + 1,)), dma((p.chips // 2, p.chips // 2)),
-            dma((p.images,)), dma((p.images,)),
+            dma((9,)), dma((3,)),
+            dma((3,)), dma((p.most + 1,)),
+            dma((1,)), dma((1,)),
+            dma((1,)), dma((1,)),
+            dma((3,)), dma((p.chips * p.most + 1,)),
+            dma((1,)), dma((2,)),
+            dma((1,)), dma((1,)),
+            dma((1,)), dma((1,)), dma((1,)),
+            dma((1,)), dma((1,)),
         ],
         compiler_params=pltpu.CompilerParams(
             collective_id=0, has_side_effects=True, vmem_limit_bytes=60 << 20
@@ -689,6 +660,11 @@
         copy = pltpu.make_async_copy(source, target, store_sem.at[len(stores)])
         copy.start()
         stores.append(copy)
+
+    whole = [
+        pltpu.make_async_copy(source, target, store_sem.at[4 + number])
+        for number, (source, target) in enumerate(((tdq_ref, tdq_out), (tdk_ref, tdk_out), (tdv_ref, tdv_out)))
+    ]
 
     load_parts.wait()
     for number in range(p.images):
@@ -720,9 +696,9 @@
             tdv_ref[0:half, lanes] = join(tback_ref, pair, slice(even, even + half), left)
             tdv_ref[half : p.text_rows, lanes] = join(tback_ref, pair, slice(even, even + p.text_rows - half), right)
         lanes = slice(step * group * width, (step + 1) * group * width)
-        for source, target in ((tdq_ref, tdq_out), (tdk_ref, tdk_out), (tdv_ref, tdv_out)):
-            store(source.at[:, lanes], target.at[:, lanes])
-    for copy in stores:
+        for number, (source, target) in enumerate(((tdq_ref, tdq_out), (tdk_ref, tdk_out), (tdv_ref, tdv_out))):
+            pltpu.make_async_copy(source.at[:, lanes], target.at[:, lanes], store_sem.at[4 + number]).start()
+    for copy in (*stores, *whole):
         copy.wait()
 
 
@@ -740,7 +716,7 @@
         scratch_shapes=[pltpu.VMEM(value.shape, value.dtype) for value in (back, tback, parts, *outs)]
         + [
             pltpu.SemaphoreType.DMA((2 + p.finish_steps,)),
-            pltpu.SemaphoreType.DMA((4 + 3 * p.finish_steps,)),
+            pltpu.SemaphoreType.DMA((7,)),
         ],
         compiler_params=pltpu.CompilerParams(vmem_limit_bytes=60 << 20),
     )(back, tback, parts)

time: 93.2 us -> 88.3 us (0.947)
  Pallas kernels: 92.1 us -> 87.2 us
    pallas_call x1, Pallas kernels: 88.4 us -> 83.5 us  [exchange(): pl.pallas_call(functools.partial(exchange_kernel, p), out_shape=(jax.Shap...]
where the time goes in v2:
time: 88.3 us; the launch traced here: 87.8 us
  Pallas kernels  87.2 us (99%)
    pallas_call x1, Pallas kernels, exchange(): pl.pallas_call(functools.partial(exchange_kernel, p), out_shape=(jax.Shap...  83.5 us
    pallas_call x1, Pallas kernels, finish(): pl.pallas_call(functools.partial(finish_kernel, p), out_shape=outs, in_sp...  3.64 us

profile of v2, /device:TPU:1, one launch (start us, length us, event | category | flops | bytes accessed | tf_op | source)
XLA Modules:
  0.0 87.8 jit_solution(12732322543222460632)
XLA Ops:
  0.6 83.5 %shard_map.180 = (bf16[20,192,128]{2,1,0:T(8,128)(2,1)}, bf16[20,512,128]{2,1,0:T(8,128)(2,1)}, bf16[4,80,1280]{2,1,0:T(8,128)(2,1)}) custom-call(bf16[128,1280]{1,0:T(8,128)(2,1)} %bitcast.24, bf16[128,1280]{1,0:T(8,128)(2,1)} %bitcast.25, bf16[128,1280]{1,0:T(8,128)(2,1)} %bitcast.26, bf16[128,1280]{1,0:T(8,128)(2,1)} %bitcast.27, ...), custom_call_target="tpu_custom_call" | custom-call | tf_op jit(solution)/shard_map/pallas_call | solution.py:587
  84.2 3.6 %shard_map.181 = (bf16[128,1280]{1,0:T(8,128)(2,1)}, bf16[128,1280]{1,0:T(8,128)(2,1)}, bf16[128,1280]{1,0:T(8,128)(2,1)}, bf16[333,1280]{1,0:T(8,128)(2,1)}, bf...) custom-call(bf16[20,192,128]{2,1,0:T(8,128)(2,1)} %get-tuple-element.17.back_in, ...), custom_call_target="tpu_custom_call" | custom-call | tf_op jit(solution)/shard_map/pallas_call | solution.py:711

commit v3 on v2

--- a/solution.py
+++ b/solution.py
@@ -631,29 +631,18 @@
             dma((1,)), dma((1,)),
         ],
         compiler_params=pltpu.CompilerParams(
-            collective_id=0, has_side_effects=True, vmem_limit_bytes=60 << 20
+            collective_id=0, has_side_effects=True, vmem_limit_bytes=44 << 20
         ),
-    )(*arrays)
+    )(*(pltpu.with_memory_space_constraint(array, pltpu.HBM) for array in arrays))
 
 
 def finish_kernel(
-    plan, back_in, tback_in, parts_in, dq_out, dk_out, dv_out, tdq_out, tdk_out, tdv_out, wg_out,
-    back_ref, tback_ref, parts_ref, dq_ref, dk_ref, dv_ref, tdq_ref, tdk_ref, tdv_ref, wg_ref,
-    load_sem, store_sem,
+    plan, back_ref, tback_ref, parts_ref, dq_out, dk_out, dv_out, tdq_out, tdk_out, tdv_out, wg_out,
+    dq_ref, dk_ref, dv_ref, tdq_ref, tdk_ref, tdv_ref, wg_ref, store_sem,
 ):
     p = plan
     width, rows, half, even = p.width, p.rows, p.text_half, p.text_even
     group = p.heads // p.finish_steps
-    text_loads = [
-        pltpu.make_async_copy(
-            tback_in.at[pl.ds(step * group, group)], tback_ref.at[pl.ds(step * group, group)], load_sem.at[2 + step]
-        )
-        for step in range(p.finish_steps)
-    ]
-    load_parts = pltpu.make_async_copy(parts_in, parts_ref, load_sem.at[0])
-    load_back = pltpu.make_async_copy(back_in, back_ref, load_sem.at[1])
-    for load in (load_parts, load_back, *text_loads):
-        load.start()
     stores = []
 
     def store(source, target):
@@ -666,7 +655,6 @@
         for number, (source, target) in enumerate(((tdq_ref, tdq_out), (tdk_ref, tdk_out), (tdv_ref, tdv_out)))
     ]
 
-    load_parts.wait()
     for number in range(p.images):
         start = p.part_start(number)
         stop = min(start + p.part, p.share)
@@ -677,7 +665,6 @@
         return jnp.concatenate([ref[2 * pair, at, cols], ref[2 * pair + 1, at, cols]], axis=1)
 
     left, right = slice(0, width), slice(width, p.depth)
-    load_back.wait()
     for pair in range(p.heads // 2):
         lanes = slice(pair * p.depth, (pair + 1) * p.depth)
         dq_ref[:, lanes] = join(back_ref, pair, slice(0, rows), left)
@@ -688,7 +675,6 @@
     store(dk_ref, dk_out)
     store(dv_ref, dv_out)
     for step in range(p.finish_steps):
-        text_loads[step].wait()
         for pair in range(step * group // 2, (step + 1) * group // 2):
             lanes = slice(pair * p.depth, (pair + 1) * p.depth)
             tdq_ref[:, lanes] = join(tback_ref, pair, slice(0, p.text_rows), left)
@@ -711,14 +697,11 @@
     return pl.pallas_call(
         functools.partial(finish_kernel, p),
         out_shape=outs,
-        in_specs=[anywhere] * 3,
+        in_specs=[pl.BlockSpec(memory_space=pltpu.VMEM)] * 3,
         out_specs=(anywhere,) * 7,
-        scratch_shapes=[pltpu.VMEM(value.shape, value.dtype) for value in (back, tback, parts, *outs)]
-        + [
-            pltpu.SemaphoreType.DMA((2 + p.finish_steps,)),
-            pltpu.SemaphoreType.DMA((7,)),
-        ],
-        compiler_params=pltpu.CompilerParams(vmem_limit_bytes=60 << 20),
+        scratch_shapes=[pltpu.VMEM(value.shape, value.dtype) for value in outs]
+        + [pltpu.SemaphoreType.DMA((7,))],
+        compiler_params=pltpu.CompilerParams(vmem_limit_bytes=24 << 20),
     )(back, tback, parts)
 
 

time: 88.3 us -> 87.1 us (0.986)
  Pallas kernels: 87.2 us -> 85.9 us
where the time goes in v3:
time: 87.1 us; the launch traced here: 86.6 us
  Pallas kernels  85.9 us (99%)
    pallas_call x1, Pallas kernels, exchange(): pl.pallas_call(functools.partial(exchange_kernel, p), out_shape=(jax.Shap...  83.1 us
    pallas_call x1, Pallas kernels, finish(): pl.pallas_call(functools.partial(finish_kernel, p), out_shape=outs, in_sp...  2.86 us

profile of v3, /device:TPU:1, one launch (start us, length us, event | category | flops | bytes accessed | tf_op | source)
XLA Modules:
  0.0 86.6 jit_solution(3417464700526958211)
XLA Ops:
  0.6 83.1 %shard_map.180 = (bf16[20,192,128]{2,1,0:T(8,128)(2,1)S(1)}, bf16[20,512,128]{2,1,0:T(8,128)(2,1)S(1)}, bf16[4,80,1280]{2,1,0:T(8,128)(2,1)S(1)}) custom-call(bf16[128,1280]{1,0:T(8,128)(2,1)} %bitcast.24, bf16[128,1280]{1,0:T(8,128)(2,1)} %bitcast.25, bf16[128,1280]{1,0:T(8,128)(2,1)} %bitcast.26, bf16[128,1280]{1,0:T(8,128)(2,1)} %bitcast.27, ...), custom_call_target="tpu_custom_call" | custom-call | tf_op jit(solution)/shard_map/pallas_call | solution.py:587
  83.7 2.9 %shard_map.181 = (bf16[128,1280]{1,0:T(8,128)(2,1)}, bf16[128,1280]{1,0:T(8,128)(2,1)}, bf16[128,1280]{1,0:T(8,128)(2,1)}, bf16[333,1280]{1,0:T(8,128)(2,1)}, bf...) custom-call(bf16[20,192,128]{2,1,0:T(8,128)(2,1)S(1)} %get-tuple-element.17.back_ref, ...), custom_call_target="tpu_custom_call" | custom-call | tf_op jit(solution)/shard_map/pallas_call | solution.py:697

commit v4 on v3

--- a/solution.py
+++ b/solution.py
@@ -330,6 +330,9 @@
     def own_back(j):
         return pltpu.make_async_copy(result_s.at[j, me], back_ref.at[first + j], own_sem.at[0])
 
+    def ordered(head, value):
+        return jnp.where(head % 2 == 1, jnp.concatenate([value[:, width:], value[:, :width]], axis=1), value)
+
     def send_back(j):
         own_back(j).start()
 
@@ -438,13 +441,13 @@
 
         dq = (dq_s[:, p.tokens : p.total].T * scaling).astype(BF)
         even, half = p.text_even, p.text_half
-        text_s[j, 0:even] = jnp.concatenate(
-            [dq[:even, :width], dk_s[p.tokens : p.tokens + even, :width]], axis=1
-        )
-        text_s[j, even : even + half] = jnp.concatenate(
+        top = jnp.concatenate([dq[:even, :width], dk_s[p.tokens : p.tokens + even, :width]], axis=1)
+        bottom = jnp.concatenate(
             [dv_s[p.tokens : p.tokens + half, :width], dv_s[p.tokens + half : p.tokens + 2 * half, :width]],
             axis=1,
         )
+        text_s[j, 0:even] = ordered(head, top)
+        text_s[j, even : even + half] = ordered(head, bottom)
         own_text(j).start()
         send_text(text_s.at[j], head, me, True, True)
 
@@ -484,8 +487,8 @@
             top = jnp.concatenate([dq[:, :width], dk_s[pl.ds(base, rows), :width]], axis=1)
             dv = dv_s[pl.ds(base, rows), :width]
             bottom = jnp.concatenate([dv[: rows // 2], dv[rows // 2 :]], axis=1)
-            result_s[j, block, 0:rows] = top
-            result_s[j, block, rows : p.out_rows] = bottom
+            result_s[j, block, 0:rows] = ordered(head, top)
+            result_s[j, block, rows : p.out_rows] = ordered(head, bottom)
 
         @pl.when(j == 0)
         def _():
@@ -661,10 +664,15 @@
         wg_ref[start:stop, :] = parts_ref[number, 0 : stop - start, :].astype(F32)
     store(wg_ref, wg_out)
 
-    def join(ref, pair, at, cols):
-        return jnp.concatenate([ref[2 * pair, at, cols], ref[2 * pair + 1, at, cols]], axis=1)
-
-    left, right = slice(0, width), slice(width, p.depth)
+    def join(ref, pair, at, left):
+        even_head, odd_head = ref[2 * pair, at, :], ref[2 * pair + 1, at, :]
+        lower = lax.broadcasted_iota(jnp.int32, even_head.shape, 1) < width
+        if left:
+            return jnp.where(lower, even_head, odd_head)
+        mixed = jnp.where(lower, odd_head, even_head)
+        return jnp.concatenate([mixed[:, width:], mixed[:, :width]], axis=1)
+
+    left, right = True, False
     for pair in range(p.heads // 2):
         lanes = slice(pair * p.depth, (pair + 1) * p.depth)
         dq_ref[:, lanes] = join(back_ref, pair, slice(0, rows), left)

time: 87.1 us -> 87.1 us (level)
  no operation moved by 1% of the time
where the time goes in v4:
time: 87.1 us; the launch traced here: 86.6 us
  Pallas kernels  85.9 us (99%)
    pallas_call x1, Pallas kernels, exchange(): pl.pallas_call(functools.partial(exchange_kernel, p), out_shape=(jax.Shap...  83.2 us
    pallas_call x1, Pallas kernels, finish(): pl.pallas_call(functools.partial(finish_kernel, p), out_shape=outs, in_sp...  2.71 us

profile of v4, /device:TPU:1, one launch (start us, length us, event | category | flops | bytes accessed | tf_op | source)
XLA Modules:
  0.0 86.6 jit_solution(17143311093833854563)
XLA Ops:
  0.6 83.2 %shard_map.180 = (bf16[20,192,128]{2,1,0:T(8,128)(2,1)S(1)}, bf16[20,512,128]{2,1,0:T(8,128)(2,1)S(1)}, bf16[4,80,1280]{2,1,0:T(8,128)(2,1)S(1)}) custom-call(bf16[128,1280]{1,0:T(8,128)(2,1)} %bitcast.24, bf16[128,1280]{1,0:T(8,128)(2,1)} %bitcast.25, bf16[128,1280]{1,0:T(8,128)(2,1)} %bitcast.26, bf16[128,1280]{1,0:T(8,128)(2,1)} %bitcast.27, ...), custom_call_target="tpu_custom_call" | custom-call | tf_op jit(solution)/shard_map/pallas_call | solution.py:590
  83.9 2.7 %shard_map.181 = (bf16[128,1280]{1,0:T(8,128)(2,1)}, bf16[128,1280]{1,0:T(8,128)(2,1)}, bf16[128,1280]{1,0:T(8,128)(2,1)}, bf16[333,1280]{1,0:T(8,128)(2,1)}, bf...) custom-call(bf16[20,192,128]{2,1,0:T(8,128)(2,1)S(1)} %get-tuple-element.17.back_ref, ...), custom_call_target="tpu_custom_call" | custom-call | tf_op jit(solution)/shard_map/pallas_call | solution.py:705

commit v5 on v4

--- a/solution.py
+++ b/solution.py
@@ -34,7 +34,7 @@
         self.total = self.tokens + up(text_rows, LANES)
         self.key_block = self.total // 8
         self.text_even = up(text_rows, SUB)
-        self.text_half = up(self.text_even // 2, SUB)
+        self.text_half = up(self.text_even // 2, 8)
         self.out_rows = rows + rows // 2
         self.out_text = self.text_even + self.text_half
         self.share = model // peers

time: 87.1 us -> 86.9 us (level)
  no operation moved by 1% of the time
where the time goes in v5:
time: 86.9 us; the launch traced here: 86.4 us
  Pallas kernels  85.8 us (99%)
    pallas_call x1, Pallas kernels, exchange(): pl.pallas_call(functools.partial(exchange_kernel, p), out_shape=(jax.Shap...  83.1 us
    pallas_call x1, Pallas kernels, finish(): pl.pallas_call(functools.partial(finish_kernel, p), out_shape=outs, in_sp...  2.71 us

profile of v5, /device:TPU:1, one launch (start us, length us, event | category | flops | bytes accessed | tf_op | source)
XLA Modules:
  0.0 86.4 jit_solution(10320388543961190200)
XLA Ops:
  0.6 83.1 %shard_map.180 = (bf16[20,192,128]{2,1,0:T(8,128)(2,1)S(1)}, bf16[20,504,128]{2,1,0:T(8,128)(2,1)S(1)}, bf16[4,80,1280]{2,1,0:T(8,128)(2,1)S(1)}) custom-call(bf16[128,1280]{1,0:T(8,128)(2,1)} %bitcast.24, bf16[128,1280]{1,0:T(8,128)(2,1)} %bitcast.25, bf16[128,1280]{1,0:T(8,128)(2,1)} %bitcast.26, bf16[128,1280]{1,0:T(8,128)(2,1)} %bitcast.27, ...), custom_call_target="tpu_custom_call" | custom-call | tf_op jit(solution)/shard_map/pallas_call | solution.py:590
  83.7 2.7 %shard_map.181 = (bf16[128,1280]{1,0:T(8,128)(2,1)}, bf16[128,1280]{1,0:T(8,128)(2,1)}, bf16[128,1280]{1,0:T(8,128)(2,1)}, bf16[333,1280]{1,0:T(8,128)(2,1)}, bf...) custom-call(bf16[20,192,128]{2,1,0:T(8,128)(2,1)S(1)} %get-tuple-element.17.back_ref, ...), custom_call_target="tpu_custom_call" | custom-call | tf_op jit(solution)/shard_map/pallas_call | solution.py:705
